TPU v7x, 16 devices: a 4x2x1 block of a 4x4x8 slice. The times are simulated.
16 devices in a mesh: rep: 2 (over y, z), dp: 8 (over x, core).
Axes of the slice: x: 4, y: 2, z: 1, core: 2. Of those that a mesh axis runs over, the one named last changes fastest.
The devices are a block of a 4x4x8 slice.
Arguments:
- x: bfloat16 [16, 2048, 768], P(('rep', 'dp')), parts along dimension 0
- dy: bfloat16 [16, 2048, 768], P(('rep', 'dp')), parts along dimension 0
- w_gate: bfloat16 [2, 768, 2304], replicated
- w_up: bfloat16 [2, 768, 2304], replicated
- w_down: bfloat16 [2, 2304, 768], replicated
- m_w_gate: float32 [2, 768, 2304], replicated
- m_w_up: float32 [2, 768, 2304], replicated
- m_w_down: float32 [2, 2304, 768], replicated
- v_w_gate: float32 [2, 768, 2304], replicated
- v_w_up: float32 [2, 768, 2304], replicated
- v_w_down: float32 [2, 2304, 768], replicated
Outputs:
- output 1: bfloat16 [4, 768, 2304], P('rep'), parts along dimension 0
- output 2: bfloat16 [4, 768, 2304], P('rep'), parts along dimension 0
- output 3: bfloat16 [4, 2304, 768], P('rep'), parts along dimension 0
- output 4: float32 [4, 768, 2304], P('rep'), parts along dimension 0
- output 5: float32 [4, 768, 2304], P('rep'), parts along dimension 0
- output 6: float32 [4, 2304, 768], P('rep'), parts along dimension 0
- output 7: float32 [4, 768, 2304], P('rep'), parts along dimension 0
- output 8: float32 [4, 768, 2304], P('rep'), parts along dimension 0
- output 9: float32 [4, 2304, 768], P('rep'), parts along dimension 0
There are 2 independent parts. A program takes and returns all parts, laid end to end along the dimension named above; an argument that names none is the same for every part.
All inputs are finite; a program needn't handle non-finite values.
Results may differ from a plain program's by a relative error of at most 0.022.
Values are sent between devices in bfloat16 or wider.
A program may use at most 768 MiB of HBM per device.

v0:
```python
import jax
import jax.numpy as jnp
from jax import lax
from jax.sharding import PartitionSpec as P

NAMES = ("w_gate", "w_up", "w_down")


def matmul(a, w):
    return jnp.dot(a, w, preferred_element_type=jnp.float32).astype(jnp.bfloat16)


def normed(h):
    wide = h.astype(jnp.float32)
    scale = lax.rsqrt(jnp.mean(wide**2, -1, keepdims=True) + 1e-6)
    return (wide * scale).astype(jnp.bfloat16)


def layer(h, w):
    a = normed(h)
    gate = jnp.dot(a, w["w_gate"], preferred_element_type=jnp.float32)
    up = jnp.dot(a, w["w_up"], preferred_element_type=jnp.float32)
    return h + matmul((jax.nn.silu(gate) * up).astype(jnp.bfloat16), w["w_down"])


def adamw(w, m, v, g):
    m = 0.9 * m + 0.1 * g
    v = 0.95 * v + 0.05 * g * g
    step = m * lax.rsqrt(v + 1e-8) + 0.1 * w
    return (w - 0.02 * step).astype(jnp.bfloat16), m, v


def clipped(gradients, sum_of_squares, count):
    factor = jnp.minimum(1.0, 0.5 * lax.rsqrt(sum_of_squares / count + 1e-30))
    return [g * factor for g in gradients]


def solution(mesh):
    def step(x, dy, *arrays):
        weights, m, v = (arrays[i : i + 3] for i in (0, 3, 6))
        layers = weights[0].shape[0]
        h, kept = x[0], []
        for number in range(layers):
            kept.append(h)
            h = layer(h, {name: w[number] for name, w in zip(NAMES, weights, strict=True)})
        by_h, summed = dy[0], [None] * layers
        for number in reversed(range(layers)):
            _, back = jax.vjp(lambda w, h: layer(h, w), {name: w[number] for name, w in zip(NAMES, weights, strict=True)}, kept[number])
            by_w, by_h = back(by_h)
            summed[number] = [lax.psum(by_w[name], "dp") for name in NAMES]
        gradients = [jnp.stack([summed[number][i] for number in range(layers)]).astype(jnp.float32) for i in range(3)]
        gradients = clipped(gradients, sum(jnp.sum(g * g) for g in gradients), sum(g.size for g in gradients))
        new = [adamw(w.astype(jnp.float32), m, v, g) for w, m, v, g in zip(weights, m, v, gradients, strict=True)]
        return tuple(one[which] for which in range(3) for one in new)

    return jax.shard_map(
        step,
        mesh=mesh,
        in_specs=(P(("rep", "dp"), None, None),) * 2 + (P(None, None, None),) * 9,
        out_specs=(P("rep", None, None),) * 9,
        check_vma=False,
    )
```

profile of v0, /device:TPU:113, one launch (start us, length us, event | category | flops | bytes accessed | tf_op | source)
XLA Modules:
  0.0 575.8 jit_solution(1420322181863904185)
XLA Ops:
  7.2 0.1 all-reduce.3.cloned.1.call-start
  7.3 3.2 copy.20
  10.5 0.0 copy-start.2
  10.5 0.7 fusion.36
  11.2 5.0 copy.21
  16.2 12.5 %convolution_convert_fusion.1 = bf16[2048,2304]{1,0:T(8,128)(2,1)} fusion(bf16[2,2304,768]{2,1,0:T(8,128)(2,1)} %param.15, bf16[1,2048,768]{2,1,0:T(8,128)(2,1)} %param.12), kind=kOutput, calls=%fused_computation.59 | convolution fusion | flops 7252475904 | bytes 16121856 | tf_op jit(solution)/shard_map/transpose(jvp())/dot_general | solution.py:10
  28.7 0.0 copy-done.5
  28.7 13.0 %fusion.70 = f32[2048,2304]{1,0:T(8,128)} fusion(bf16[2,768,2304]{2,1,0:T(8,128)(2,1)} %param.13, bf16[1,2048,768]{2,1,0:T(8,128)(2,1)S(1)} %copy-done.5, f32[2048]{0:T(1024)S(1)} %add_rsqrt_fusion), kind=kOutput, calls=%fused_computation.105 | convolution fusion | flops 7252475904 | bytes 25567232 | tf_op jit(solution)/shard_map/dot_general | solution.py:21
  41.7 0.0 copy-done.11
  41.7 19.0 %multiply_convert_fusion.1 = (bf16[2048,2304]{1,0:T(8,128)(2,1)}, f32[2048,2304]{1,0:T(8,128)}) fusion(f32[2048,2304]{1,0:T(8,128)} %fusion.70, bf16[2,768,2304]{2,1,0:T(8,128)(2,1)} %param.14, bf16[1,2048,768]{2,1,0:T(8,128)(2,1)} %param.11, f32[2048]{0:T(1024)S(1)} %add_rsqrt_fusion), kind=kOutput, calls=%fused_computation.20 | convolution fusion | flops 7280787456 | bytes 53878784 | tf_op jit(solution)/shard_map/dot_general | solution.py:22
  60.7 0.0 copy-done.2
  60.7 11.9 %fusion.40 = (f32[2048]{0:T(1024)S(1)}, bf16[2048,768]{0,1:T(8,128)(2,1)S(1)}) fusion(bf16[2048,2304]{1,0:T(8,128)(2,1)} %get-tuple-element.24, bf16[2,2304,768]{2,1,0:T(8,128)(2,1)} %param.15, bf16[1,2048,768]{1,2,0:T(8,128)(2,1)S(1)} %copy.20), kind=kOutput, calls=%fused_computation.76 | convolution fusion | flops 7255619584 | bytes 19275776 | tf_op jit(solution)/shard_map/dot_general | solution.py:10
  72.5 0.0 copy-start.9
  72.6 0.0 copy-start.7
  72.6 0.6 copy-done.9
  73.1 1.1 copy-done.7
  74.2 13.5 %fusion.57 = f32[2048,2304]{1,0:T(8,128)} fusion(bf16[2,768,2304]{2,1,0:T(8,128)(2,1)} %param.14, bf16[2048,768]{0,1:T(8,128)(2,1)S(1)} %get-tuple-element.27, f32[2048]{0:T(1024)S(1)} %fusion.108), kind=kOutput, calls=%fused_computation.92 | convolution fusion | flops 7252475904 | bytes 25567232 | tf_op jit(solution)/shard_map/jvp()/dot_general | solution.py:22
  87.8 30.5 %fusion.2 = (bf16[2048,2304]{1,0:T(8,128)(2,1)}, f32[2048,2304]{1,0:T(8,128)}) fusion(f32[2048,2304]{1,0:T(8,128)} %fusion.57, bf16[2048,2304]{1,0:T(8,128)(2,1)} %convolution_convert_fusion.1, bf16[2,768,2304]{2,1,0:T(8,128)(2,1)} %param.13, bf16[2048,768]{0,1:T(8,128)(2,1)} %copy-done.7, f32[2048]{0:T(1024)S(1)} %fusion.108), kind=kOutput, calls=%fused_computation.11 | convolution fusion | flops 7309099008 | bytes 63315968 | tf_op jit(solution)/shard_map/jvp()/dot_general | solution.py:21
  118.3 0.0 slice-done.2
  118.3 0.0 slice-done.3
  118.3 0.0 copy-start.8
  118.3 0.0 copy-start.13
  118.3 11.3 %fusion.78 = bf16[2048,768]{0,1:T(8,128)(2,1)} fusion(bf16[2048,2304]{1,0:T(8,128)(2,1)} %get-tuple-element.28, bf16[2,768,2304]{2,1,0:T(8,128)(2,1)S(1)} %bitcast.83), kind=kOutput, calls=%fused_computation.111 | convolution fusion | flops 7247757312 | bytes 16121856 | tf_op jit(solution)/shard_map/transpose(jvp())/dot_general | solution.py:21
  129.7 0.0 copy-done.8
  129.7 0.0 copy-done.13
  129.7 8.9 %fusion.50 = bf16[1,768,2304]{2,1,0:T(8,128)(2,1)} fusion(bf16[2048,2304]{1,0:T(8,128)(2,1)S(1)} %copy-done.13, bf16[2048,768]{0,1:T(8,128)(2,1)S(1)} %copy-done.8, f32[2048]{0:T(1024)S(1)} %fusion.108), kind=kOutput, calls=%fused_computation.87 | convolution fusion | flops 7252475904 | bytes 16130048 | tf_op jit(solution)/shard_map/transpose(jvp())/dot_general | solution.py:21
  138.6 0.0 copy-done.6
  138.6 18.0 %fusion.49 = bf16[1,2304,768]{2,1,0:T(8,128)(2,1)} fusion(f32[2048,2304]{1,0:T(8,128)} %fusion.57, bf16[1,2048,768]{2,1,0:T(8,128)(2,1)S(1)} %copy-done.6, f32[2048,2304]{1,0:T(8,128)} %get-tuple-element.29), kind=kOutput, calls=%fused_computation.86 | convolution fusion | flops 7277838336 | bytes 44433408 | tf_op jit(solution)/shard_map/transpose(jvp())/dot_general | solution.py:10
  156.6 16.4 %fusion.56 = bf16[1,768,2304]{2,1,0:T(8,128)(2,1)} fusion(bf16[2048,2304]{1,0:T(8,128)(2,1)} %convolution_convert_fusion.1, bf16[2048,768]{0,1:T(8,128)(2,1)} %copy-done.7, f32[2048]{0:T(1024)S(1)} %fusion.108, f32[2048,2304]{1,0:T(8,128)} %get-tuple-element.29), kind=kOutput, calls=%fused_computation.91 | convolution fusion | flops 7282556928 | bytes 35004416 | tf_op jit(solution)/shard_map/transpose(jvp())/dot_general | solution.py:22
  173.0 19.6 %fusion.42 = (f32[2048]{0:T(1024)S(1)}, bf16[2048,768]{0,1:T(8,128)(2,1)}) fusion(bf16[2048,768]{0,1:T(8,128)(2,1)} %copy-done.7, bf16[2048,768]{0,1:T(8,128)(2,1)} %fusion.78, bf16[2,768,2304]{2,1,0:T(8,128)(2,1)} %param.14, bf16[2048,2304]{1,0:T(8,128)(2,1)} %convolution_convert_fusion.1, f32[2048,2304]{1,0:T(8,128)} %get-tuple-element.29), kind=kOutput, calls=%fused_computation.78 | convolution fusion | flops 7285504000 | bytes 41295872 | tf_op jit(solution)/shard_map/transpose(jvp())/dot_general | solution.py:22
  192.6 0.0 copy-done.4
  192.6 0.0 slice-start
  192.6 5.2 fusion.86
  197.8 0.0 slice-start.1
  197.9 11.6 %fusion.51 = bf16[1,2304,768]{2,1,0:T(8,128)(2,1)} fusion(bf16[2048,2304]{1,0:T(8,128)(2,1)} %get-tuple-element.24, bf16[2048,768]{0,1:T(8,128)(2,1)S(1)} %fusion.86), kind=kOutput, calls=%fused_computation.88 | convolution fusion | flops 7249526784 | bytes 16121856 | tf_op jit(solution)/shard_map/transpose(jvp())/dot_general | solution.py:10
  209.5 0.0 copy-start.12
  209.5 10.2 %convolution_convert_fusion = bf16[2048,2304]{1,0:T(8,128)(2,1)} fusion(bf16[2048,768]{0,1:T(8,128)(2,1)S(1)} %fusion.86, bf16[2,2304,768]{2,1,0:T(8,128)(2,1)S(1)} %bitcast.81), kind=kOutput, calls=%fused_computation.58 | convolution fusion | flops 7252475904 | bytes 16121856 | tf_op jit(solution)/shard_map/transpose(jvp())/dot_general | solution.py:10
  219.7 0.0 copy-done.3
  219.7 15.6 %fusion.52 = bf16[1,768,2304]{2,1,0:T(8,128)(2,1)} fusion(bf16[2048,2304]{1,0:T(8,128)(2,1)} %convolution_convert_fusion, f32[2048,2304]{1,0:T(8,128)} %fusion.70, bf16[1,2048,768]{1,2,0:T(8,128)(2,1)S(1)} %copy-done.3, f32[2048]{0:T(1024)S(1)} %copy-done.12), kind=kOutput, calls=%fused_computation.89 | convolution fusion | flops 7282556928 | bytes 35004416 | tf_op jit(solution)/shard_map/transpose(jvp())/dot_general | solution.py:22
  235.3 20.4 %fusion.53 = bf16[1,768,2304]{2,1,0:T(8,128)(2,1)} fusion(f32[2048,2304]{1,0:T(8,128)} %fusion.70, f32[2048,2304]{1,0:T(8,128)} %get-tuple-element.25, bf16[2048,2304]{1,0:T(8,128)(2,1)} %convolution_convert_fusion, bf16[1,2048,768]{1,2,0:T(8,128)(2,1)S(1)} %copy-done.3, f32[2048]{0:T(1024)S(1)} %copy-done.12), kind=kOutput, calls=%fused_computation.90 | convolution fusion | flops 7306149888 | bytes 53878784 | tf_op jit(solution)/shard_map/transpose(jvp())/dot_general | solution.py:21
  255.7 0.1 all-reduce.3.cloned.1.call-update
  255.8 219.3 %all-reduce.3.cloned.1.call-done = (bf16[1,768,2304]{2,1,0:T(8,128)(2,1)}, bf16[1,768,2304]{2,1,0:T(8,128)(2,1)}, bf16[1,768,2304]{2,1,0:T(8,128)(2,1)}, bf16[1,...) async-done(((bf16[1,768,2304]{2,1,0:T(8,128)(2,1)}, bf16[1,768,2304]{2,1,0:T(8,128)(2,1)}, bf16[1,768,2304]{2,1,0:T(8,128)(2,1)}, ...) | async-done | bytes 21233680 | tf_op jit(solution)/shard_map/psum | solution.py:50
  475.1 7.5 %fusion.22 = f32[]{:T(128)} fusion(bf16[1,2304,768]{2,1,0:T(8,128)(2,1)} %get-tuple-element.13, bf16[1,2304,768]{2,1,0:T(8,128)(2,1)} %get-tuple-element.14), kind=kLoop, calls=%fused_computation.46 | loop fusion | flops 14155775 | bytes 7077892 | tf_op jit(solution)/shard_map/reduce_sum | solution.py:52
  482.6 7.3 %fusion.21 = f32[]{:T(128)} fusion(bf16[1,768,2304]{2,1,0:T(8,128)(2,1)} %get-tuple-element.11, bf16[1,768,2304]{2,1,0:T(8,128)(2,1)} %get-tuple-element.12), kind=kLoop, calls=%fused_computation.45 | loop fusion | flops 14155775 | bytes 7077892 | tf_op jit(solution)/shard_map/reduce_sum | solution.py:52
  489.9 0.0 copy-done.1
  489.9 4.2 fusion.20
  496.1 24.8 %fusion.28 = (bf16[2,2304,768]{2,1,0:T(8,128)(2,1)}, f32[2,2304,768]{2,1,0:T(8,128)}, f32[2,2304,768]{2,1,0:T(8,128)}) fusion(bf16[2,2304,768]{2,1,0:T(8,128)(2,1)} %param.15, f32[]{:T(128)S(6)} %min_shard_map.3, bf16[1,2304,768]{2,1,0:T(8,128)(2,1)} %get-tuple-element.13, bf16[1,2304,768]{2,1,0:T(8,128)(2,1)} %get-tuple-element.14, ...), kind=kLoop, calls=%fused_computation.52 | loop fusion | flops 70778880 | bytes 77856768 | tf_op jit(solution)/shard_map/convert_element_type | solution.py:30
  520.9 47.5 %fusion.19 = (bf16[2,768,2304]{2,1,0:T(8,128)(2,1)}, f32[2,768,2304]{2,1,0:T(8,128)}, f32[2,768,2304]{2,1,0:T(8,128)}, bf16[2,768,2304]{2,1,0:T(8,128)(2,1)}, f3...) fusion(bf16[2,768,2304]{2,1,0:T(8,128)(2,1)} %param.13, f32[]{:T(128)S(6)} %min_shard_map.3, ...), kind=kLoop, calls=%fused_computation.43 | loop fusion | flops 141557760 | bytes 155713536 | tf_op jit(solution)/shard_map/convert_element_type | solution.py:30
  (20 shorter events, 0.1 us)
Async XLA Ops:
  7.2 467.9 %all-reduce.3.cloned.1.call-start = ((), (), s32[]{:S(2)}) async-start(), calls=%async_computation | async-start | bytes 42467328 | tf_op jit(solution)/shard_map/psum | solution.py:50
  10.5 50.2 %copy-start.2 = (bf16[1,2048,768]{1,2,0:T(8,128)(2,1)}, bf16[1,2048,768]{1,2,0:T(8,128)(2,1)S(1)}, u32[]{:S(2)}) copy-start(bf16[1,2048,768]{1,2,0:T(8,128)(2,1)S(1)} %copy.20) | copy-start | bytes 9437188
  11.1 30.6 %copy-start.11 = (f32[2048]{0:T(1024)}, f32[2048]{0:T(1024)S(1)}, u32[]{:S(2)}) copy-start(f32[2048]{0:T(1024)S(1)} %add_rsqrt_fusion) | copy-start | bytes 24580
  16.2 12.6 %copy-start.5 = (bf16[1,2048,768]{2,1,0:T(8,128)(2,1)S(1)}, bf16[1,2048,768]{2,1,0:T(8,128)(2,1)}, u32[]{:S(2)}) copy-start(bf16[1,2048,768]{2,1,0:T(8,128)(2,1)} %param.11) | copy-start | bytes 9437188
  72.5 0.6 copy-start.9
  72.6 1.7 copy-start.7
  74.2 44.1 %slice-start.2 = ((s8[7077888]{0:T(1024)(128)(4,1)}), s8[4194304]{0:T(1024)(128)(4,1)S(1)}, s32[]{:S(2)}) async-start(s8[7077888]{0:T(1024)(128)(4,1)} %bitcast.82), calls=%async_computation.3 | async-start | bytes 8388608
  87.8 30.5 %slice-start.3 = ((s8[7077888]{0:T(1024)(128)(4,1)}), s8[2883584]{0:T(1024)(128)(4,1)S(1)}, s32[]{:S(2)}) async-start(s8[7077888]{0:T(1024)(128)(4,1)} %bitcast.82), calls=%async_computation.4 | async-start | bytes 5767168
  118.3 11.4 %copy-start.8 = (bf16[2048,768]{0,1:T(8,128)(2,1)S(1)}, bf16[2048,768]{0,1:T(8,128)(2,1)}, u32[]{:S(2)}) copy-start(bf16[2048,768]{0,1:T(8,128)(2,1)} %copy-done.7) | copy-start | bytes 9437188
  118.3 11.3 %copy-start.13 = (bf16[2048,2304]{1,0:T(8,128)(2,1)S(1)}, bf16[2048,2304]{1,0:T(8,128)(2,1)}, u32[]{:S(2)}) copy-start(bf16[2048,2304]{1,0:T(8,128)(2,1)} %get-tuple-element.28) | copy-start | bytes 28311556
  129.7 8.9 %copy-start.6 = (bf16[1,2048,768]{2,1,0:T(8,128)(2,1)S(1)}, bf16[1,2048,768]{2,1,0:T(8,128)(2,1)}, u32[]{:S(2)}) copy-start(bf16[1,2048,768]{2,1,0:T(8,128)(2,1)} %param.12) | copy-start | bytes 9437188
  173.0 19.6 %copy-start.10 = (f32[2048]{0:T(1024)S(1)}, f32[2048]{0:T(1024)}, u32[]{:S(2)}) copy-start(f32[2048]{0:T(1024)} %copy-done.9) | copy-start | bytes 24580
  173.0 19.6 %copy-start.4 = (bf16[1,2048,768]{1,2,0:T(8,128)(2,1)S(1)}, bf16[1,2048,768]{1,2,0:T(8,128)(2,1)}, u32[]{:S(2)}) copy-start(bf16[1,2048,768]{1,2,0:T(8,128)(2,1)} %copy.21) | copy-start | bytes 9437188
  192.6 16.8 %slice-start = ((s8[7077888]{0:T(1024)(128)(4,1)}), s8[4194304]{0:T(1024)(128)(4,1)S(1)}, s32[]{:S(2)}) async-start(s8[7077888]{0:T(1024)(128)(4,1)} %bitcast.80), calls=%async_computation.1 | async-start | bytes 8388608
  197.8 11.6 %slice-start.1 = ((s8[7077888]{0:T(1024)(128)(4,1)}), s8[2883584]{0:T(1024)(128)(4,1)S(1)}, s32[]{:S(2)}) async-start(s8[7077888]{0:T(1024)(128)(4,1)} %bitcast.80), calls=%async_computation.2 | async-start | bytes 5767168
  209.4 10.2 %copy-start.3 = (bf16[1,2048,768]{1,2,0:T(8,128)(2,1)S(1)}, bf16[1,2048,768]{1,2,0:T(8,128)(2,1)}, u32[]{:S(2)}) copy-start(bf16[1,2048,768]{1,2,0:T(8,128)(2,1)} %copy-done.2) | copy-start | bytes 9437188
  209.5 10.2 %copy-start.12 = (f32[2048]{0:T(1024)S(1)}, f32[2048]{0:T(1024)}, u32[]{:S(2)}) copy-start(f32[2048]{0:T(1024)} %copy-done.11) | copy-start | bytes 24580
  475.1 14.8 %copy-start = (bf16[1,768,2304]{2,1,0:T(8,128)(2,1)S(1)}, bf16[1,768,2304]{2,1,0:T(8,128)(2,1)}, u32[]{:S(2)}) copy-start(bf16[1,768,2304]{2,1,0:T(8,128)(2,1)} %get-tuple-element.9) | copy-start | bytes 10616836
  475.1 14.8 %copy-start.1 = (bf16[1,768,2304]{2,1,0:T(8,128)(2,1)S(1)}, bf16[1,768,2304]{2,1,0:T(8,128)(2,1)}, u32[]{:S(2)}) copy-start(bf16[1,768,2304]{2,1,0:T(8,128)(2,1)} %get-tuple-element.10) | copy-start | bytes 10616836
Sparse Core Ops, SparseCore 0:
  255.9 219.1 all-reduce.2
where the time goes:
time: 584 us; the launch traced here: 576 us
  matrix products  232 us (40%)
  waiting for transfers between devices  219 us (38%)
  other arithmetic  97.2 us (17%)
  between operations  16.7 us (3%)
  local copies, waits for them, and re-layouts  9.94 us (2%)
    psum x1, waiting for transfers between devices, step(): summed[number] = [lax.psum(by_w[name], 'dp') for name in NAMES]  219 us
    dot_general x5, matrix products, layer(): gate = jnp.dot(a, w['w_gate'], preferred_element_type=jnp.float32)  84.2 us
    dot_general x5, matrix products, layer(): up = jnp.dot(a, w['w_up'], preferred_element_type=jnp.float32)  84 us
    convert_element_type x2, other arithmetic, adamw(): return ((w - 0.02 * step).astype(jnp.bfloat16), m, v)  72.3 us
    dot_general x5, matrix products, matmul(): jnp.dot(a, w, preferred_element_type=jnp.float32).astype(jnp.bfloat16)  64.2 us
    reduce_sum x3, other arithmetic, step(): jnp.sum(g * g)  19 us
  transfers between devices with their start and end apart: 1, of which 1 were waited for; matrix products, arithmetic and copies ran while one was open for 0% of the time, Pallas kernels for 0%

commit v1 on v0

v1 whole, which is shorter than its diff:
```python
import functools

import jax
import jax.numpy as jnp
from jax import lax
from jax.experimental import pallas as pl
from jax.experimental.pallas import tpu as pltpu
from jax.sharding import PartitionSpec as P

F32, BF16 = jnp.float32, jnp.bfloat16
WIDTH = 256
CHUNK = 512
VMEM_LIMIT = 60 * 1024 * 1024
NT = (((1,), (1,)), ((), ()))


def dot(a, b):
    return jnp.dot(a, b, preferred_element_type=F32)


def dot_nt(a, b):
    return lax.dot_general(a, b, NT, preferred_element_type=F32)


def normed(h):
    wide = h.astype(F32)
    scale = lax.rsqrt(jnp.mean(wide**2, -1, keepdims=True) + 1e-6)
    return (wide * scale).astype(BF16)


def forward_kernel(a_ref, h_ref, wg_ref, wu_ref, wd_ref, out_ref, acc):
    s = pl.program_id(0)
    tokens = a_ref.shape[0]

    @pl.when(s == 0)
    def _():
        acc[...] = jnp.zeros_like(acc)

    def body(t, _):
        rows = pl.ds(pl.multiple_of(t * CHUNK, CHUNK), CHUNK)
        a = a_ref[rows, :]
        gate = dot(a, wg_ref[0])
        up = dot(a, wu_ref[0])
        act = (gate * jax.nn.sigmoid(gate) * up).astype(BF16)
        acc[rows, :] += dot(act, wd_ref[0])
        return 0

    lax.fori_loop(0, tokens // CHUNK, body, 0)

    @pl.when(s == pl.num_programs(0) - 1)
    def _():
        out_ref[...] = h_ref[...] + acc[...].astype(BF16)


def forward(layer, a, h, wg, wu, wd):
    tokens, d = a.shape
    ff = wg.shape[-1]
    whole = pl.BlockSpec((tokens, d), lambda s: (0, 0))
    return pl.pallas_call(
        forward_kernel,
        grid=(ff // WIDTH,),
        in_specs=[
            whole,
            whole,
            pl.BlockSpec((1, d, WIDTH), lambda s: (layer, 0, s)),
            pl.BlockSpec((1, d, WIDTH), lambda s: (layer, 0, s)),
            pl.BlockSpec((1, WIDTH, d), lambda s: (layer, s, 0)),
        ],
        out_specs=whole,
        out_shape=jax.ShapeDtypeStruct((tokens, d), BF16),
        scratch_shapes=[pltpu.VMEM((tokens, d), F32)],
        compiler_params=pltpu.CompilerParams(vmem_limit_bytes=VMEM_LIMIT, dimension_semantics=("arbitrary",)),
        name="forward",
    )(a, h, wg, wu, wd)


def backward_kernel(with_da, a_ref, at_ref, dy_ref, dyt_ref, wg_ref, wu_ref, wd_ref, g_ref, da_ref, gu_buf, act_buf, acc):
    s = pl.program_id(0)
    tokens, d = a_ref.shape

    if with_da:

        @pl.when(s == 0)
        def _():
            acc[...] = jnp.zeros_like(acc)

    def body(t, _):
        rows = pl.ds(pl.multiple_of(t * CHUNK, CHUNK), CHUNK)
        a = a_ref[rows, :]
        gate = dot(a, wg_ref[0])
        up = dot(a, wu_ref[0])
        dact = dot_nt(dy_ref[rows, :], wd_ref[0]).astype(BF16).astype(F32)
        sig = jax.nn.sigmoid(gate)
        silu = gate * sig
        act_buf[rows, :] = (silu * up).astype(BF16)
        dup = (dact * silu).astype(BF16)
        dgate = (dact * up * (sig + silu * (1 - sig))).astype(BF16)
        gu_buf[rows, :WIDTH] = dgate
        gu_buf[rows, WIDTH:] = dup
        if with_da:
            acc[rows, :] += dot_nt(dgate, wg_ref[0]) + dot_nt(dup, wu_ref[0])
        return 0

    lax.fori_loop(0, tokens // CHUNK, body, 0)

    def weights(i, _):
        rows = pl.ds(pl.multiple_of(i * 256, 256), 256)
        both = dot(at_ref[rows, :], gu_buf[...]).astype(BF16)
        g_ref[0, pl.ds(pl.multiple_of(i * 256, 256), 256), :] = both[:, :WIDTH]
        g_ref[0, pl.ds(pl.multiple_of(d + i * 256, 256), 256), :] = both[:, WIDTH:]
        g_ref[0, pl.ds(pl.multiple_of(2 * d + i * 256, 256), 256), :] = dot(dyt_ref[rows, :], act_buf[...]).astype(BF16)
        return 0

    lax.fori_loop(0, d // 256, weights, 0)

    if with_da:

        @pl.when(s == pl.num_programs(0) - 1)
        def _():
            da_ref[...] = acc[...].astype(BF16)


def backward(layer, with_da, a, dy, wg, wu, wd):
    tokens, d = a.shape
    ff = wg.shape[-1]
    whole = pl.BlockSpec((tokens, d), lambda s: (0, 0))
    wholet = pl.BlockSpec((d, tokens), lambda s: (0, 0))
    da_rows = tokens if with_da else 8
    return pl.pallas_call(
        functools.partial(backward_kernel, with_da),
        grid=(ff // WIDTH,),
        in_specs=[
            whole,
            wholet,
            whole,
            wholet,
            pl.BlockSpec((1, d, WIDTH), lambda s: (layer, 0, s)),
            pl.BlockSpec((1, d, WIDTH), lambda s: (layer, 0, s)),
            pl.BlockSpec((1, WIDTH, d), lambda s: (layer, s, 0)),
        ],
        out_specs=[
            pl.BlockSpec((1, 3 * d, WIDTH), lambda s: (s, 0, 0)),
            pl.BlockSpec((da_rows, d), lambda s: (0, 0)),
        ],
        out_shape=[
            jax.ShapeDtypeStruct((ff // WIDTH, 3 * d, WIDTH), BF16),
            jax.ShapeDtypeStruct((da_rows, d), BF16),
        ],
        scratch_shapes=[
            pltpu.VMEM((tokens, 2 * WIDTH), BF16),
            pltpu.VMEM((tokens, WIDTH), BF16),
            pltpu.VMEM((da_rows, d), F32),
        ],
        compiler_params=pltpu.CompilerParams(vmem_limit_bytes=VMEM_LIMIT, dimension_semantics=("arbitrary",)),
        name="backward",
    )(a, a.T, dy, dy.T, wg, wu, wd)


def norm_backward(h, da, dh):
    _, back = jax.vjp(normed, h)
    return dh + back(da)[0]


def adamw_kernel(f_ref, g0_ref, g1_ref, *refs):
    ws, ms, vs = refs[0:3], refs[3:6], refs[6:9]
    new_ws, new_ms, new_vs = refs[9:12], refs[12:15], refs[15:18]
    factor = f_ref[0]
    d = ws[0].shape[1]
    layer = pl.program_id(0)

    def update(g, w, m, v, new_w, new_m, new_v, rows, columns):
        at = (0, rows, columns)
        g = g.astype(F32) * factor
        m = 0.9 * m[at] + 0.1 * g
        v = 0.95 * v[at] + 0.05 * g * g
        new_m[at] = m
        new_v[at] = v
        wide = w[at].astype(F32)
        new_w[at] = (wide - 0.02 * (m * lax.rsqrt(v + 1e-8) + 0.1 * wide)).astype(BF16)

    def take(g_ref):
        for i in range(2):
            for j in range(d // 256):
                rows = slice(j * 256, (j + 1) * 256)
                update(g_ref[0, i * d + j * 256 : i * d + (j + 1) * 256, :], *(r[i] for r in (ws, ms, vs, new_ws, new_ms, new_vs)), rows, slice(None))
        for j in range(d // 256):
            g = g_ref[0, 2 * d + j * 256 : 2 * d + (j + 1) * 256, :].astype(F32).T
            update(g, *(r[2] for r in (ws, ms, vs, new_ws, new_ms, new_vs)), slice(None), slice(j * 256, (j + 1) * 256))

    @pl.when(layer == 0)
    def _():
        take(g0_ref)

    @pl.when(layer != 0)
    def _():
        take(g1_ref)


def adamw(factor, g, weights, m, v):
    layers, d, ff = weights[0].shape
    n = ff // WIDTH
    wide = pl.BlockSpec((1, d, WIDTH), lambda l, s: (l, 0, s))
    tall = pl.BlockSpec((1, WIDTH, d), lambda l, s: (l, s, 0))
    three = [wide, wide, tall]
    return pl.pallas_call(
        adamw_kernel,
        grid=(layers, n),
        in_specs=[
            pl.BlockSpec(memory_space=pltpu.SMEM),
            pl.BlockSpec((1, 3 * d, WIDTH), lambda l, s: (jnp.where(l == 0, s, n - 1), 0, 0)),
            pl.BlockSpec((1, 3 * d, WIDTH), lambda l, s: (jnp.where(l == 0, 0, s), 0, 0)),
        ]
        + three * 3,
        out_specs=three * 3,
        out_shape=[jax.ShapeDtypeStruct(w.shape, t) for t in (BF16, F32, F32) for w in weights],
        compiler_params=pltpu.CompilerParams(vmem_limit_bytes=VMEM_LIMIT, dimension_semantics=("arbitrary", "arbitrary")),
        name="adamw",
    )(factor, *g, *weights, *m, *v)


def solution(mesh):
    def step(x, dy, *arrays):
        weights, m, v = (arrays[i : i + 3] for i in (0, 3, 6))
        layers = weights[0].shape[0]
        h, kept = x[0], []
        for number in range(layers):
            a = normed(h)
            kept.append((h, a))
            if number < layers - 1:
                h = forward(number, a, h, *weights)
        by_h, g = dy[0], [None] * layers
        for number in reversed(range(layers)):
            h, a = kept[number]
            part, da = backward(number, number > 0, a, by_h, *weights)
            g[number] = lax.psum(part, "dp")
            if number > 0:
                by_h = norm_backward(h, da, by_h)
        squares = sum(jnp.sum(one.astype(F32) ** 2) for one in g)
        count = sum(one.size for one in g)
        factor = jnp.minimum(1.0, 0.5 * lax.rsqrt(squares / count + 1e-30))
        return tuple(adamw(factor.reshape(1), g, weights, m, v))

    return jax.shard_map(
        step,
        mesh=mesh,
        in_specs=(P(("rep", "dp"), None, None),) * 2 + (P(None, None, None),) * 9,
        out_specs=(P("rep", None, None),) * 9,
        check_vma=False,
    )
```

time: 584 us -> 589 us (level); the launches traced: 576 us -> 588 us
  Pallas kernels: 0 us -> 294 us
  matrix products: 232 us -> 0 us
  other arithmetic: 97.2 us -> 29.1 us
  local copies, waits for them, and re-layouts: 9.94 us -> 30 us
    pallas_call x0 -> x4, Pallas kernels: none -> 294 us  [the longest x2 170 us: backward(): pl.pallas_call(functools.partial(backward_kernel, with_da), grid=(ff // W...]
    dot_general x15 -> x0, matrix products: 232 us -> none  [the longest x5 84.2 us: layer(): gate = jnp.dot(a, w['w_gate'], preferred_element_type=jnp.float32)]
    convert_element_type x2, other arithmetic: 72.3 us -> 4.88 us  [normed(): return (wide * scale).astype(BF16)]
    convert_element_type x0 -> x2, local copies, waits for them, and re-layouts: none -> 9.26 us  [normed(): return (wide * scale).astype(BF16)]
    pallas_call x0 -> x2, local copies, waits for them, and re-layouts: none -> 7.82 us  [the longest x1 4.63 us: backward(): pl.pallas_call(functools.partial(backward_kernel, with_da), grid=(ff // W...]
    reduce_sum x3 -> x2, other arithmetic: 19 us -> 14.1 us  [the longest x1 10.7 us: step(): squares = sum((jnp.sum(one.astype(F32) ** 2) for one in g))]
where the time goes in v1:
time: 589 us; the launch traced here: 588 us
  Pallas kernels  294 us (50%)
  waiting for transfers between devices  219 us (37%)
  local copies, waits for them, and re-layouts  30 us (5%)
  other arithmetic  29.1 us (5%)
  between operations  15.5 us (3%)
    psum x1, waiting for transfers between devices, step(): g[number] = lax.psum(part, 'dp')  219 us
    pallas_call x2, Pallas kernels, backward(): pl.pallas_call(functools.partial(backward_kernel, with_da), grid=(ff // W...  170 us
    pallas_call x1, Pallas kernels, adamw(): pl.pallas_call(adamw_kernel, grid=(layers, n), in_specs=[pl.BlockSpec(mem...  85.6 us
    pallas_call x1, Pallas kernels, forward(): pl.pallas_call(forward_kernel, grid=(ff // WIDTH,), in_specs=[whole, whol...  38.6 us
  transfers between devices with their start and end apart: 1, of which 1 were waited for; matrix products, arithmetic and copies ran while one was open for 0% of the time, Pallas kernels for 0%

profile of v1, /device:TPU:113, one launch (start us, length us, event | category | flops | bytes accessed | tf_op | source)
XLA Modules:
  0.0 588.3 jit_solution(9856100260457610334)
XLA Ops:
  7.2 0.1 all-reduce.3.cloned.1.call-start
  7.3 3.2 copy.20
  10.5 0.7 fusion
  11.1 2.4 fusion.10.at_ref
  13.6 2.4 fusion.1
  16.0 4.6 copy.28.a_ref
  20.6 38.6 %forward.1 = bf16[2048,768]{1,0:T(8,128)(2,1)} custom-call(bf16[2048,768]{1,0:T(8,128)(2,1)} %copy.28.a_ref, bf16[2048,768]{1,0:T(8,128)(2,1)} %bitcast.19, bf16[2,768,2304]{2,1,0:T(8,128)(2,1)} %refs_0_.1, bf16[2,768,2304]{2,1,0:T(8,128)(2,1)} %refs_1_.1, bf16[2,2304,768]{2,1,0:T(8,128)(2,1)} %refs_2_.1), custom_call_target="tpu_custom_call" | custom-call | tf_op jit(solution)/shard_map/forward/pallas_call | solution.py:59
  59.3 3.2 copy.24
  62.4 0.7 fusion.4
  63.1 2.4 fusion.9.at_ref
  65.6 2.4 fusion.5
  68.0 4.6 copy.21
  72.6 4.6 copy.25.a_ref
  77.3 107.4 %backward.2 = (bf16[9,2304,256]{2,1,0:T(8,128)(2,1)}, bf16[2048,768]{1,0:T(8,128)(2,1)}) custom-call(bf16[2048,768]{1,0:T(8,128)(2,1)} %copy.25.a_ref, bf16[768,2048]{1,0:T(8,128)(2,1)} %fusion.9.at_ref, bf16[2048,768]{1,0:T(8,128)(2,1)} %bitcast.20, bf16[768,2048]{1,0:T(8,128)(2,1)} %bitcast.17, bf16[2,768,2304]{2,1,0:T(8,128)(2,1)} %refs_0_.1, ...), custom_call_target="tpu_custom_call" | custom-call | tf_op jit(solution)/shard_map/backward/pallas_call | solution.py:129
  184.6 4.6 copy.27
  189.3 0.0 copy-start
  189.3 0.0 copy-start.1
  189.3 3.3 fusion.6
  192.6 0.0 copy-done
  192.6 0.4 copy-done.1
  193.1 3.9 fusion.7
  197.0 4.6 copy.29.dy_ref
  201.6 62.8 %backward.3 = (bf16[9,2304,256]{2,1,0:T(8,128)(2,1)}, bf16[8,768]{1,0:T(8,128)(2,1)}) custom-call(bf16[2048,768]{1,0:T(8,128)(2,1)} %copy.28.a_ref, bf16[768,2048]{1,0:T(8,128)(2,1)} %fusion.10.at_ref, bf16[2048,768]{1,0:T(8,128)(2,1)} %copy.29.dy_ref, bf16[768,2048]{1,0:T(8,128)(2,1)} %bitcast.18, bf16[2,768,2304]{2,1,0:T(8,128)(2,1)} %refs_0_.1, ...), custom_call_target="tpu_custom_call" | custom-call | tf_op jit(solution)/shard_map/backward/pallas_call | solution.py:129
  264.4 0.1 all-reduce.3.cloned.1.call-update
  264.5 219.2 %all-reduce.3.cloned.1.call-done = (bf16[9,2304,256]{2,1,0:T(8,128)(2,1)}, bf16[9,2304,256]{2,1,0:T(8,128)(2,1)}) async-done(((bf16[9,2304,256]{2,1,0:T(8,128)(2,1)}, bf16[9,2304,256]{2,1,0:T(8,128)(2,1)}), (bf16[9,2304,256]{2,1,0:T(8,128)(2,1)}, bf16[9,2304,256]{2,1,0:T(8,128)(2,1)})) %all-reduce.3.cloned.1.call-update) | async-done | bytes 21233680 | tf_op jit(solution)/shard_map/psum | solution.py:235
  483.7 10.7 %multiply_reduce_fusion = (f32[]{:T(128)}, f32[]{:T(128)}) fusion(bf16[9,2304,256]{2,1,0:T(8,128)(2,1)} %get-tuple-element.16.g1_ref, bf16[9,2304,256]{2,1,0:T(8,128)(2,1)} %get-tuple-element.15.g0_ref), kind=kLoop, calls=%fused_computation | loop fusion | flops 31850496 | bytes 21233672 | tf_op jit(solution)/shard_map/reduce_sum | solution.py:238
  495.8 85.6 %adamw.1 = (bf16[2,768,2304]{2,1,0:T(8,128)(2,1)}, bf16[2,768,2304]{2,1,0:T(8,128)(2,1)}, bf16[2,2304,768]{2,1,0:T(8,128)(2,1)}, f32[2,768,2304]{2,1,0:T(8,128)}...) custom-call(f32[1]{0:T(128)} %bitcast.8.f_ref, ...), custom_call_target="tpu_custom_call" | custom-call | tf_op jit(solution)/shard_map/adamw/pallas_call | solution.py:205
  (3 shorter events, 0.0 us)
Async XLA Ops:
  7.2 476.5 %all-reduce.3.cloned.1.call-start = ((), (), s32[]{:S(2)}) async-start(), calls=%async_computation | async-start | bytes 42467328 | tf_op jit(solution)/shard_map/psum | solution.py:235
  189.3 3.3 copy-start
  189.3 3.8 copy-start.1
Sparse Core Ops, SparseCore 0:
  264.6 219.0 all-reduce.2

commit v2 on v0

v2 whole, which is shorter than its diff:
```python
import functools

import jax
import jax.numpy as jnp
from jax import lax
from jax.experimental import pallas as pl
from jax.experimental.pallas import tpu as pltpu
from jax.sharding import PartitionSpec as P

F32, BF16 = jnp.float32, jnp.bfloat16
MESH = pl.DeviceIdType.MESH
WIDTH = 768
STRIP = 256
CHUNK = 512
ROWS = 256
VMEM_LIMIT = 63 * 1024 * 1024
NT = (((1,), (1,)), ((), ()))


def dot(a, b):
    return jnp.dot(a, b, preferred_element_type=F32)


def dot_nt(a, b):
    return lax.dot_general(a, b, NT, preferred_element_type=F32)


def norm_scale(wide):
    return lax.rsqrt(jnp.mean(wide**2, -1, keepdims=True) + 1e-6)


def normed(h):
    wide = h.astype(F32)
    return (wide * norm_scale(wide)).astype(BF16)


def once(shape):
    return pl.BlockSpec(shape, lambda *_: (0,) * len(shape), pipeline_mode=pl.Buffered(1))


def forward_kernel(h_ref, wg_ref, wu_ref, wd_ref, out_ref, a_buf, acc):
    s = pl.program_id(0)
    tokens = a_buf.shape[0]
    chunks = [pl.ds(t, CHUNK) for t in range(0, tokens, CHUNK)]

    @pl.when(s == 0)
    def _():
        for rows in chunks:
            a_buf[rows, :] = normed(h_ref[0, rows, :])
            acc[rows, :] = jnp.zeros((CHUNK, acc.shape[1]), F32)

    for rows in chunks:
        a = a_buf[rows, :]
        gate = dot(a, wg_ref[0])
        up = dot(a, wu_ref[0])
        act = (gate * jax.nn.sigmoid(gate) * up).astype(BF16)
        acc[rows, :] += dot(act, wd_ref[0])

    @pl.when(s == pl.num_programs(0) - 1)
    def _():
        for rows in chunks:
            out_ref[0, rows, :] = h_ref[0, rows, :] + acc[rows, :].astype(BF16)


def weight_specs(layer, d):
    wide = pl.BlockSpec((1, d, WIDTH), lambda s: (layer, 0, s))
    return [wide, wide, pl.BlockSpec((1, WIDTH, d), lambda s: (layer, s, 0))]


def forward(layer, h, weights):
    _, tokens, d = h.shape
    ff = weights[0].shape[-1]
    return pl.pallas_call(
        forward_kernel,
        grid=(ff // WIDTH,),
        in_specs=[once(h.shape)] + weight_specs(layer, d),
        out_specs=once(h.shape),
        out_shape=jax.ShapeDtypeStruct(h.shape, BF16),
        scratch_shapes=[pltpu.VMEM((tokens, d), BF16), pltpu.VMEM((tokens, d), F32)],
        compiler_params=pltpu.CompilerParams(vmem_limit_bytes=VMEM_LIMIT, dimension_semantics=("arbitrary",)),
        name="forward",
    )(h, *weights)


class Exchange:
    def __init__(self, n, g_buf, got_half, got_far, got_near, own_ref, squares, sems):
        self.g_buf, self.got_half, self.got_far, self.got_near = g_buf, got_half, got_far, got_near
        self.own_ref, self.squares = own_ref, squares
        self.swap_sems, self.sems = sems
        me = lax.axis_index("dp")
        self.core, self.chip = lax.rem(me, 2), me // 2
        self.chips = n // 2
        self.right = lax.rem(self.chip + 1, self.chips)
        self.left = lax.rem(self.chip + self.chips - 1, self.chips)
        self.far = lax.rem(self.chip + 2, self.chips)
        self.share = got_near.shape[2]

    def to(self, chip, core):
        return {"dp": chip * 2 + core}

    def barrier(self):
        barrier = pltpu.get_barrier_semaphore()
        peers = [(self.chip, 1 - self.core), (self.right, self.core), (self.left, self.core)]
        for peer in peers:
            pl.semaphore_signal(barrier, inc=1, device_id=self.to(*peer), device_id_type=MESH)
        pl.semaphore_wait(barrier, len(peers))

    def swap(self, u, slot):
        rows = self.share * self.chips
        other = pl.ds(pl.multiple_of((1 - self.core) * rows, rows), rows)
        return pltpu.make_async_remote_copy(
            src_ref=self.g_buf.at[slot, other],
            dst_ref=self.got_half.at[u],
            send_sem=self.swap_sems.at[0, u],
            recv_sem=self.swap_sems.at[1, u],
            device_id=self.to(self.chip, 1 - self.core),
            device_id_type=MESH,
        )

    def at(self, slot, chip, top=True, bottom=True):
        start = (self.core * self.chips + chip) * self.share + (0 if top else self.share // 2)
        size = self.share if top and bottom else self.share // 2
        return self.g_buf.at[slot, pl.ds(pl.multiple_of(start, size), size)]

    def copy(self, u, slot, which):
        top, bottom = pl.ds(0, self.share // 2), pl.ds(self.share // 2, self.share // 2)
        source, target, chip = {
            0: (self.at(slot, self.far, bottom=False), self.got_far.at[u, 0], self.right),
            1: (self.at(slot, self.far, top=False), self.got_far.at[u, 1], self.left),
            2: (self.at(slot, self.right, top=False), self.got_near.at[u, 0, bottom], self.right),
            3: (self.at(slot, self.left, bottom=False), self.got_near.at[u, 1, top], self.left),
            4: (self.at(slot, self.right, bottom=False), self.got_near.at[u, 0, top], self.right),
            5: (self.at(slot, self.left, top=False), self.got_near.at[u, 1, bottom], self.left),
        }[which]
        return pltpu.make_async_remote_copy(
            src_ref=source,
            dst_ref=target,
            send_sem=self.sems.at[0, u, which],
            recv_sem=self.sems.at[1, u, which],
            device_id=self.to(chip, self.core),
            device_id_type=MESH,
        )

    def first(self, u, slot):
        self.swap(u, slot).wait()
        for chip in range(self.chips):
            there = pl.ds(chip * self.share, self.share)
            mine = self.at(slot, chip)
            mine[...] = (mine[...].astype(F32) + self.got_half[u, there, :].astype(F32)).astype(BF16)
        for which in range(4):
            self.copy(u, slot, which).start()

    def second(self, u, slot):
        for which, mine in ((0, self.at(slot, self.right, bottom=False)), (1, self.at(slot, self.left, top=False))):
            self.copy(u, slot, which).wait_recv()
            mine[...] = (mine[...].astype(F32) + self.got_far[u, which].astype(F32)).astype(BF16)
            self.copy(u, slot, which + 4).start()

    def third(self, u, slot):
        for which in range(2, 6):
            self.copy(u, slot, which).wait_recv()
        total = self.at(slot, self.chip)[...].astype(F32) + self.got_near[u, 0].astype(F32) + self.got_near[u, 1].astype(F32)
        total = total.astype(BF16)
        self.own_ref[u] = total
        wide = total.astype(F32)
        wide = (wide * wide).reshape(-1, 8, wide.shape[-1]).sum(0)
        self.squares[...] += sum(wide[:, i : i + 128] for i in range(0, wide.shape[-1], 128))
        for which in range(6):
            self.copy(u, slot, which).wait_send()


def backward_kernel(n, with_da, h_ref, dy_ref, wg_ref, wu_ref, wd_ref, *refs):
    outs = 3 if with_da else 2
    own_ref, squares_ref = refs[0], refs[1]
    a_buf, at_buf, dyt_buf, gu_buf, act_buf, acc = refs[outs : outs + 6]
    g_buf, got_half, got_far, got_near, *sems = refs[outs + 6 :]
    s = pl.program_id(0)
    last = pl.num_programs(0) - 1
    tokens, d = a_buf.shape
    chunks = [pl.ds(t, CHUNK) for t in range(0, tokens, CHUNK)]
    ex = Exchange(n, g_buf, got_half, got_far, got_near, own_ref, squares_ref, sems)

    @pl.when(s == 0)
    def _():
        ex.barrier()
        squares_ref[...] = jnp.zeros_like(squares_ref)
        for rows in chunks:
            a = normed(h_ref[0, rows, :])
            a_buf[rows, :] = a
            at_buf[:, rows] = a.T
            dyt_buf[:, rows] = dy_ref[0, rows, :].T
            if with_da:
                acc[rows, :] = jnp.zeros((CHUNK, d), F32)

    before = 3 * (s - 1)

    def tick(t):
        @pl.when(s > 0)
        def _():
            if t == 0:
                ex.first(before + 2, 2)
                ex.second(before, 0)
            if t == 1:
                ex.second(before + 1, 1)
            if t == 2:
                ex.second(before + 2, 2)
                ex.third(before, 0)
            if t == 3:
                ex.third(before + 1, 1)
                ex.third(before + 2, 2)

    for t, rows in enumerate(chunks):
        tick(t)
        a = a_buf[rows, :]
        gate = dot(a, wg_ref[0])
        up = dot(a, wu_ref[0])
        dact = dot_nt(dy_ref[0, rows, :], wd_ref[0]).astype(BF16).astype(F32)
        sig = jax.nn.sigmoid(gate)
        silu = gate * sig
        act_buf[rows, :] = (silu * up).astype(BF16)
        dup = (dact * silu).astype(BF16)
        dgate = (dact * up * (sig + silu * (1 - sig))).astype(BF16)
        gu_buf[0, rows, :] = dgate
        gu_buf[1, rows, :] = dup
        if with_da:
            acc[rows, :] += dot_nt(dgate, wg_ref[0]) + dot_nt(dup, wu_ref[0])

    for j, (left, right) in enumerate(((at_buf, gu_buf.at[0]), (at_buf, gu_buf.at[1]), (dyt_buf, act_buf))):

        def weights(i, _):
            rows = pl.ds(pl.multiple_of(i * ROWS, ROWS), ROWS)
            g_buf[j, rows, :] = dot(left[rows, :], right[...]).astype(BF16)
            return 0

        lax.fori_loop(0, d // ROWS, weights, 0)
        ex.swap(3 * s + j, j).start()
        if j > 0:
            ex.first(3 * s + j - 1, j - 1)

    @pl.when(s == last)
    def _():
        u = 3 * s
        ex.first(u + 2, 2)
        ex.second(u, 0)
        if with_da:
            dh_ref = refs[2]
            for rows in chunks:
                wide = h_ref[0, rows, :].astype(F32)
                scale = norm_scale(wide)
                da = acc[rows, :].astype(BF16).astype(F32)
                by_h = da * scale - wide * (scale * scale * scale * jnp.mean(da * wide, -1, keepdims=True))
                dh_ref[0, rows, :] = dy_ref[0, rows, :] + by_h.astype(BF16)
        ex.second(u + 1, 1)
        ex.second(u + 2, 2)
        for j in range(3):
            ex.third(u + j, j)


def backward(n, layer, with_da, h, dy, weights):
    _, tokens, d = h.shape
    ff = weights[0].shape[-1]
    units = 3 * (ff // WIDTH)
    share, chips = d // n, n // 2
    out_shape = [jax.ShapeDtypeStruct((units, share, WIDTH), BF16), jax.ShapeDtypeStruct((8, 128), F32)]
    if with_da:
        out_shape.append(jax.ShapeDtypeStruct(h.shape, BF16))
    return pl.pallas_call(
        functools.partial(backward_kernel, n, with_da),
        grid=(ff // WIDTH,),
        in_specs=[once(h.shape), once(h.shape)] + weight_specs(layer, d),
        out_specs=[once(o.shape) for o in out_shape],
        out_shape=out_shape,
        scratch_shapes=[
            pltpu.VMEM((tokens, d), BF16),
            pltpu.VMEM((d, tokens), BF16),
            pltpu.VMEM((d, tokens), BF16),
            pltpu.VMEM((2, tokens, WIDTH), BF16),
            pltpu.VMEM((tokens, WIDTH), BF16),
            pltpu.VMEM((tokens, d) if with_da else (8, 128), F32),
            pltpu.VMEM((3, d, WIDTH), BF16),
            pltpu.VMEM((units, chips * share, WIDTH), BF16),
            pltpu.VMEM((units, 2, share // 2, WIDTH), BF16),
            pltpu.VMEM((units, 2, share, WIDTH), BF16),
            pltpu.SemaphoreType.DMA((2, units)),
            pltpu.SemaphoreType.DMA((2, units, 6)),
        ],
        compiler_params=pltpu.CompilerParams(
            vmem_limit_bytes=VMEM_LIMIT, dimension_semantics=("arbitrary",), collective_id=1 + layer, has_side_effects=True
        ),
        name=f"backward_{layer}",
    )(h, dy, *weights)


def adamw_kernel(f_ref, g_ref, *refs):
    ws, ms, vs = refs[0:3], refs[3:6], refs[6:9]
    new_ws, new_ms, new_vs = refs[9:12], refs[12:15], refs[15:18]
    factor = f_ref[0]
    n, _, share, _ = g_ref.shape

    def update(g, w, m, v, new_w, new_m, new_v, rows, columns):
        at = (0, rows, columns)
        g = g * factor
        m = 0.9 * m[at] + 0.1 * g
        v = 0.95 * v[at] + 0.05 * g * g
        new_m[at] = m
        new_v[at] = v
        wide = w[at].astype(F32)
        new_w[at] = (wide - 0.02 * (m * lax.rsqrt(v + 1e-8) + 0.1 * wide)).astype(BF16)

    everything = list(zip(ws, ms, vs, new_ws, new_ms, new_vs, strict=True))
    place = {i: ((i % 2) * (n // 2) + i // 2) * share for i in range(n)}
    for j in range(2):
        for i, row in place.items():
            update(g_ref[i, j].astype(F32), *everything[j], slice(row, row + share), slice(None))
    order = sorted(place, key=place.get)
    half = n // 2
    for i in range(0, n, half):
        part = jnp.concatenate([g_ref[k, 2] for k in order[i : i + half]], 0).astype(F32)
        update(part.T, *everything[2], slice(None), slice(i * share, (i + half) * share))


def adamw(factor, layer, g, weights, m, v, earlier):
    layers, d, ff = weights[0].shape
    n, units, share, _ = g.shape
    wide = pl.BlockSpec((1, d, STRIP), lambda s: (layer, 0, s))
    tall = pl.BlockSpec((1, STRIP, d), lambda s: (layer, s, 0))
    three = [wide, wide, tall]
    strips = WIDTH // STRIP
    anywhere = [pl.BlockSpec(memory_space=pl.ANY)] * len(earlier)

    def kernel(f_ref, g_ref, *refs):
        adamw_kernel(f_ref, g_ref, *refs[:9], *refs[9 + len(earlier) :])

    return pl.pallas_call(
        kernel,
        grid=(ff // STRIP,),
        in_specs=[pl.BlockSpec(memory_space=pltpu.SMEM), pl.BlockSpec((n, 3, share, STRIP), lambda s: (0, s // strips, 0, s % strips))] + three * 3 + anywhere,
        out_specs=three * 3,
        out_shape=[jax.ShapeDtypeStruct(w.shape, t) for t in (BF16, F32, F32) for w in weights],
        input_output_aliases={11 + i: i for i in range(len(earlier))},
        compiler_params=pltpu.CompilerParams(vmem_limit_bytes=VMEM_LIMIT, dimension_semantics=("arbitrary",)),
        name=f"adamw_{layer}",
    )(factor, g, *weights, *m, *v, *earlier)


def solution(mesh):
    n = mesh.shape["dp"]

    def step(x, dy, *arrays):
        weights, m, v = (arrays[i : i + 3] for i in (0, 3, 6))
        layers = weights[0].shape[0]
        kept = [x]
        for number in range(layers - 1):
            kept.append(forward(number, kept[-1], weights))
        by_h, own, squares = dy, [None] * layers, []
        for number in reversed(range(layers)):
            own[number], part, *rest = backward(n, number, number > 0, kept[number], by_h, weights)
            squares.append(part)
            if rest:
                by_h = rest[0]
        count = sum(w.size for w in weights)
        total = lax.psum(sum(jnp.sum(part) for part in squares), "dp")
        factor = jnp.minimum(1.0, 0.5 * lax.rsqrt(total / count + 1e-30)).reshape(1)
        new = []
        for number in reversed(range(layers)):
            g = lax.all_gather(own[number], "dp")
            new = adamw(factor, number, g, weights, m, v, new)
        return tuple(new)

    return jax.shard_map(
        step,
        mesh=mesh,
        in_specs=(P(("rep", "dp"), None, None),) * 2 + (P(None, None, None),) * 9,
        out_specs=(P("rep", None, None),) * 9,
        check_vma=False,
    )
```

time: 584 us -> 382 us (0.65)
  Pallas kernels: 0 us -> 342 us
  matrix products: 232 us -> 0 us
  waiting for transfers between devices: 219 us -> 0.15 us
  other arithmetic: 97.2 us -> 1.89 us
  blocking collectives: 0 us -> 14 us
  local copies, waits for them, and re-layouts: 9.94 us -> 0.01 us
    pallas_call x0 -> x5, Pallas kernels: none -> 342 us  [the longest x2 232 us: backward(): pl.pallas_call(functools.partial(backward_kernel, n, with_da), grid=(ff /...]
    dot_general x15 -> x0, matrix products: 232 us -> none  [the longest x5 84.2 us: layer(): gate = jnp.dot(a, w['w_gate'], preferred_element_type=jnp.float32)]
    psum x1 -> x0, waiting for transfers between devices: 219 us -> none  [step(): summed[number] = [lax.psum(by_w[name], 'dp') for name in NAMES]]
    convert_element_type x2 -> x0, other arithmetic: 72.3 us -> none  [adamw(): return ((w - 0.02 * step).astype(jnp.bfloat16), m, v)]
    reduce_sum x4 -> x2, other arithmetic: 19.7 us -> 1.89 us  [step(): total = lax.psum(sum((jnp.sum(part) for part in squares)), 'dp')]
    psum x0 -> x1, blocking collectives: none -> 14 us  [step(): total = lax.psum(sum((jnp.sum(part) for part in squares)), 'dp')]
    unnamed x38 -> x2, local copies, waits for them, and re-layouts: 9.94 us -> 0.01 us
  transfers between devices with their start and end apart: 1 -> 2, of which waited for: 1 -> 0; matrix products, arithmetic and copies ran while one was open for 0% -> 1% of each run, Pallas kernels for 0% -> 40%
where the time goes in v2:
time: 382 us; the launch traced here: 375 us
  Pallas kernels  342 us (90%)
  between operations  16.4 us (4%)
  blocking collectives  14 us (4%)
    pallas_call x2, Pallas kernels, backward(): pl.pallas_call(functools.partial(backward_kernel, n, with_da), grid=(ff /...  232 us
    pallas_call x2, Pallas kernels, adamw(): pl.pallas_call(kernel, grid=(ff // STRIP,), in_specs=[pl.BlockSpec(memory...  80.5 us
    pallas_call x1, Pallas kernels, forward(): pl.pallas_call(forward_kernel, grid=(ff // WIDTH,), in_specs=[once(h.shap...  29.8 us
    psum x1, blocking collectives, step(): total = lax.psum(sum((jnp.sum(part) for part in squares)), 'dp')  14 us
  transfers between devices with their start and end apart: 2, of which 0 were waited for; matrix products, arithmetic and copies ran while one was open for 1% of the time, Pallas kernels for 40%

profile of v2, /device:TPU:113, one launch (start us, length us, event | category | flops | bytes accessed | tf_op | source)
XLA Modules:
  0.0 375.0 jit_solution(9406871716407975999)
XLA Ops:
  7.2 0.1 all-gather.7.cloned.1.call-start
  7.3 29.8 %forward.1.h_ref = bf16[1,2048,768]{2,1,0:T(8,128)(2,1)} custom-call(bf16[1,2048,768]{2,1,0:T(8,128)(2,1)} %h_ref.3, bf16[2,768,2304]{2,1,0:T(8,128)(2,1)} %refs_0_.3, bf16[2,768,2304]{2,1,0:T(8,128)(2,1)} %refs_1_.3, bf16[2,2304,768]{2,1,0:T(8,128)(2,1)} %refs_2_.3), custom_call_target="tpu_custom_call" | custom-call | tf_op jit(solution)/shard_map/forward/pallas_call | solution.py:73
  37.1 123.1 %backward_1.1 = (bf16[9,96,768]{2,1,0:T(8,128)(2,1)}, f32[8,128]{1,0:T(8,128)}, bf16[1,2048,768]{2,1,0:T(8,128)(2,1)}) custom-call(bf16[1,2048,768]{2,1,0:T(8,128)(2,1)} %forward.1.h_ref, bf16[1,2048,768]{2,1,0:T(8,128)(2,1)} %dy_ref.1, bf16[2,768,2304]{2,1,0:T(8,128)(2,1)} %refs_0_.3, bf16[2,768,2304]{2,1,0:T(8,128)(2,1)} %refs_1_.3, ...), custom_call_target="tpu_custom_call" | custom-call | tf_op jit(solution)/shard_map/backward_1/pallas_call | solution.py:267
  160.2 0.1 all-gather.7.cloned.1.call-update
  160.2 0.1 all-gather.5.cloned.1.call-start
  160.3 0.0 copy-start
  160.3 109.0 %backward_0.1 = (bf16[9,96,768]{2,1,0:T(8,128)(2,1)}, f32[8,128]{1,0:T(8,128)}) custom-call(bf16[1,2048,768]{2,1,0:T(8,128)(2,1)} %h_ref.3, bf16[1,2048,768]{2,1,0:T(8,128)(2,1)} %get-tuple-element.24.dy_ref, bf16[2,768,2304]{2,1,0:T(8,128)(2,1)} %refs_0_.3, bf16[2,768,2304]{2,1,0:T(8,128)(2,1)} %refs_1_.3, bf16[2,2304,768]{2,1,0:T(8,128)(2,1)} %refs_2_.3), custom_call_target="tpu_custom_call" | custom-call | tf_op jit(solution)/shard_map/backward_0/pallas_call | solution.py:267
  269.3 0.1 all-gather.5.cloned.1.call-update
  269.4 0.0 copy-done
  269.4 0.6 reduce_sum.18
  270.0 1.3 reduce_sum.19
  272.6 14.0 %psum.7 = f32[]{:T(128)} all-reduce(f32[]{:T(128)S(6)} %add.8), channel_id=1, replica_groups=mesh['rep'=2,'dp'=8] {'dp'}, use_global_device_ids=true, to_apply=%region_2.0 | all-reduce | flops 1 | bytes 8 | tf_op jit(solution)/shard_map/psum | solution.py:362
  287.3 0.0 all-gather.7.cloned.1.call-done
  287.4 40.2 %adamw_1.1 = (bf16[2,768,2304]{2,1,0:T(8,128)(2,1)}, bf16[2,768,2304]{2,1,0:T(8,128)(2,1)}, bf16[2,2304,768]{2,1,0:T(8,128)(2,1)}, f32[2,768,2304]{2,1,0:T(8,128...) custom-call(f32[1]{0:T(128)} %bitcast.f_ref, ...), custom_call_target="tpu_custom_call" | custom-call | tf_op jit(solution)/shard_map/adamw_1/pallas_call | solution.py:334
  327.6 0.0 all-gather.5.cloned.1.call-done
  327.7 40.2 %adamw_0.1 = (bf16[2,768,2304]{2,1,0:T(8,128)(2,1)}, bf16[2,768,2304]{2,1,0:T(8,128)(2,1)}, bf16[2,2304,768]{2,1,0:T(8,128)(2,1)}, f32[2,768,2304]{2,1,0:T(8,128...) custom-call(f32[1]{0:T(128)} %bitcast.f_ref, ...), custom_call_target="tpu_custom_call", output_to_operand_aliasing={{0}: (11, {}), {1}: (12, {}), {2}: (13, {}), {3}: (14, {}),... | custom-call | tf_op jit(solution)/shard_map/adamw_0/pallas_call | solution.py:334
Async XLA Ops:
  7.2 280.2 %all-gather.7.cloned.1.call-start = ((), (), s32[]{:S(2)}) async-start(), calls=%async_computation.1 | async-start | bytes 11943936 | tf_op jit(solution)/shard_map/all_gather | solution.py:366
  160.2 167.4 %all-gather.5.cloned.1.call-start = ((), (), s32[]{:S(2)}) async-start(), calls=%async_computation | async-start | bytes 11943936 | tf_op jit(solution)/shard_map/all_gather | solution.py:366
  160.3 109.1 %copy-start = (f32[8,128]{1,0:T(8,128)S(1)}, f32[8,128]{1,0:T(8,128)}, u32[]{:S(2)}) copy-start(f32[8,128]{1,0:T(8,128)} %get-tuple-element.23) | copy-start | bytes 12292
Sparse Core Ops, SparseCore 0:
  160.3 72.6 all-gather.6
  269.5 56.1 all-gather.4

commit v3 on v2

--- a/solution.py
+++ b/solution.py
@@ -93,14 +93,17 @@
         self.right = lax.rem(self.chip + 1, self.chips)
         self.left = lax.rem(self.chip + self.chips - 1, self.chips)
         self.far = lax.rem(self.chip + 2, self.chips)
+        self.row = (self.core * self.chips + self.chip) * got_near.shape[2]
         self.share = got_near.shape[2]
 
     def to(self, chip, core):
         return {"dp": chip * 2 + core}
 
-    def barrier(self):
+    def barrier(self, far):
         barrier = pltpu.get_barrier_semaphore()
         peers = [(self.chip, 1 - self.core), (self.right, self.core), (self.left, self.core)]
+        if far:
+            peers.append((self.far, self.core))
         for peer in peers:
             pl.semaphore_signal(barrier, inc=1, device_id=self.to(*peer), device_id_type=MESH)
         pl.semaphore_wait(barrier, len(peers))
@@ -169,133 +172,285 @@
             self.copy(u, slot, which).wait_send()
 
 
+class Gather:
+    def __init__(self, ex, own_ref, first, g_ref, sems, local_sem):
+        self.ex, self.own_ref, self.first, self.g_ref, self.sems, self.local_sem = ex, own_ref, first, g_ref, sems, local_sem
+
+    def rows(self, u, chip, top=True, bottom=True):
+        ex = self.ex
+        start = (ex.core * ex.chips + chip) * ex.share + (0 if top else ex.share // 2)
+        size = ex.share if top and bottom else ex.share // 2
+        return self.g_ref.at[u, pl.ds(pl.multiple_of(start, size), size)]
+
+    def copy(self, u, which):
+        ex = self.ex
+        here = (ex.chip, 1 - ex.core)
+        mine = self.rows(u, ex.chip)
+        source, target, to = {
+            0: (self.own_ref.at[self.first + u], mine, (ex.right, ex.core)),
+            1: (self.own_ref.at[self.first + u], mine, (ex.left, ex.core)),
+            2: (self.own_ref.at[self.first + u], mine, here),
+            3: (self.rows(u, ex.left, bottom=False),) * 2 + ((ex.right, ex.core),),
+            4: (self.rows(u, ex.right, top=False),) * 2 + ((ex.left, ex.core),),
+            5: (self.rows(u, ex.left),) * 2 + (here,),
+            6: (self.rows(u, ex.right),) * 2 + (here,),
+            7: (self.rows(u, ex.far, bottom=False),) * 2 + (here,),
+            8: (self.rows(u, ex.far, top=False),) * 2 + (here,),
+        }[which]
+        return pltpu.make_async_remote_copy(
+            src_ref=source,
+            dst_ref=target,
+            send_sem=self.sems.at[0, u, which],
+            recv_sem=self.sems.at[1, u, which],
+            device_id=ex.to(*to),
+            device_id_type=MESH,
+        )
+
+    def local(self, u):
+        return pltpu.make_async_copy(self.own_ref.at[self.first + u], self.rows(u, self.ex.chip), self.local_sem.at[u])
+
+    def one(self, u):
+        for which in range(3):
+            self.copy(u, which).start()
+        self.local(u).start()
+
+    def two(self, u):
+        for which in range(2):
+            self.copy(u, which).wait_recv()
+            self.copy(u, which + 3).start()
+            self.copy(u, which + 5).start()
+
+    def three(self, u):
+        for which in range(2):
+            self.copy(u, which + 3).wait_recv()
+            self.copy(u, which + 7).start()
+
+    def four(self, u):
+        for which in (2, 5, 6, 7, 8):
+            self.copy(u, which).wait_recv()
+        for which in range(9):
+            self.copy(u, which).wait_send()
+        self.local(u).wait()
+
+
+def squares_over_group(ex, squares_ref, slots, sems):
+    def send(slot, which, chip, core):
+        return pltpu.make_async_remote_copy(
+            src_ref=slots.at[slot],
+            dst_ref=slots.at[5 if which == 0 else 1 + ex.chip],
+            send_sem=sems.at[0, which],
+            recv_sem=sems.at[1, which],
+            device_id=ex.to(chip, core),
+            device_id_type=MESH,
+        )
+
+    slots[0] = squares_ref[...]
+    swap = send(0, 0, ex.chip, 1 - ex.core)
+    swap.start()
+    swap.wait()
+    slots[1 + ex.chip] = slots[0] + slots[5]
+    copies = [send(1 + ex.chip, 1 + i, chip, ex.core) for i, chip in enumerate((ex.right, ex.left, ex.far))]
+    for copy in copies:
+        copy.start()
+    for copy in copies:
+        copy.wait()
+    total = slots[1]
+    for chip in range(1, ex.chips):
+        total = total + slots[1 + chip]
+    squares_ref[...] = total
+
+
 def backward_kernel(n, with_da, h_ref, dy_ref, wg_ref, wu_ref, wd_ref, *refs):
-    outs = 3 if with_da else 2
-    own_ref, squares_ref = refs[0], refs[1]
-    a_buf, at_buf, dyt_buf, gu_buf, act_buf, acc = refs[outs : outs + 6]
-    g_buf, got_half, got_far, got_near, *sems = refs[outs + 6 :]
+    if with_da:
+        own_ref, squares_ref, gathered_ref, dh_ref, *refs = refs
+    else:
+        earlier_own_ref, earlier_squares_ref, own_ref, squares_ref, gathered_ref, *refs = refs
+    a_buf, t_buf, gu_buf, acc, g_buf, got_half, got_far, got_near, slots, *sems = refs
+    swap_sems, copy_sems, gather_sems, local_sems, slot_sems = sems
     s = pl.program_id(0)
     last = pl.num_programs(0) - 1
     tokens, d = a_buf.shape
-    chunks = [pl.ds(t, CHUNK) for t in range(0, tokens, CHUNK)]
-    ex = Exchange(n, g_buf, got_half, got_far, got_near, own_ref, squares_ref, sems)
+    steps = tokens // CHUNK
+    ex = Exchange(n, g_buf, got_half, got_far, got_near, own_ref, squares_ref, (swap_sems, copy_sems))
+    gather = Gather(ex, own_ref if with_da else earlier_own_ref, 0, gathered_ref, gather_sems, local_sems)
+
+    def chunk(t):
+        return pl.ds(pl.multiple_of(t * CHUNK, CHUNK), CHUNK)
+
+    def each(f, start=0):
+        lax.fori_loop(0, 3, lambda j, _: (f(start + j), 0)[1], 0)
 
     @pl.when(s == 0)
     def _():
-        ex.barrier()
-        squares_ref[...] = jnp.zeros_like(squares_ref)
-        for rows in chunks:
+        ex.barrier(not with_da)
+        if with_da:
+            squares_ref[...] = jnp.zeros_like(squares_ref)
+        else:
+            squares_ref[...] = earlier_squares_ref[...]
+            each(gather.one)
+
+        def prepare(t, _):
+            rows = chunk(t)
             a = normed(h_ref[0, rows, :])
             a_buf[rows, :] = a
-            at_buf[:, rows] = a.T
-            dyt_buf[:, rows] = dy_ref[0, rows, :].T
+            t_buf[0, :, rows] = a.T
+            t_buf[1, :, rows] = dy_ref[0, rows, :].T
             if with_da:
                 acc[rows, :] = jnp.zeros((CHUNK, d), F32)
-
-    before = 3 * (s - 1)
-
-    def tick(t):
-        @pl.when(s > 0)
+            return 0
+
+        lax.fori_loop(0, steps, prepare, 0)
+
+    def due(u, what):
+        steps = {"f": ex.first, "s": ex.second, "t": ex.third}
+        gathers = {"1": gather.one, "2": gather.two, "3": gather.three, "4": gather.four}
+        for step, j in zip(what[::2], map(int, what[1::2])):
+            if step in steps:
+                steps[step](u + j, j)
+            else:
+                gathers[step](u + j)
+
+    here, before = 3 * s, 3 * (s - 1)
+
+    def when(condition, *actions):
+        @pl.when(condition)
         def _():
-            if t == 0:
-                ex.first(before + 2, 2)
-                ex.second(before, 0)
-            if t == 1:
-                ex.second(before + 1, 1)
-            if t == 2:
-                ex.second(before + 2, 2)
-                ex.third(before, 0)
-            if t == 3:
-                ex.third(before + 1, 1)
-                ex.third(before + 2, 2)
-
-    for t, rows in enumerate(chunks):
-        tick(t)
+            for action in actions:
+                action()
+
+    if with_da:
+        in_hidden = {0: "s1", 1: "s2", 2: "t010", 3: "t111"}
+        in_weights = {0: "t212", 1: "20", 2: "21"}
+        in_da = {1: "f2", 2: "s0"}
+        before_in_da = {0: "2230", 2: "31"}
+        earlier_in_hidden = {0: "32", 3: "404142"}
+        at_last, before_at_last = "s1s2t0t1t2", "32404142"
+    else:
+        in_hidden = {1: "f2s0", 2: "s1"}
+        in_weights = {0: "s2t0", 1: "t1", 2: "t2"}
+        earlier_in_hidden = {}
+        at_last = "s0f2s1t0s2t1t2"
+
+    def hidden(t, _):
+        for i, what in in_hidden.items():
+            when((s > 0) & (t == i), functools.partial(due, before, what))
+        for i, what in earlier_in_hidden.items():
+            when((s > 1) & (t == i), functools.partial(due, before - 3, what))
+        if not with_da:
+            when((s == 0) & (t == 1), functools.partial(due, 0, "20"))
+            when((s == 0) & (t == 2), functools.partial(due, 0, "21"))
+            when((s == 0) & (t == 3), functools.partial(due, 0, "2230"))
+            when((s == 1) & (t == 0), functools.partial(due, 0, "3132404142"))
+        rows = chunk(t)
         a = a_buf[rows, :]
         gate = dot(a, wg_ref[0])
         up = dot(a, wu_ref[0])
         dact = dot_nt(dy_ref[0, rows, :], wd_ref[0]).astype(BF16).astype(F32)
         sig = jax.nn.sigmoid(gate)
         silu = gate * sig
-        act_buf[rows, :] = (silu * up).astype(BF16)
-        dup = (dact * silu).astype(BF16)
-        dgate = (dact * up * (sig + silu * (1 - sig))).astype(BF16)
-        gu_buf[0, rows, :] = dgate
-        gu_buf[1, rows, :] = dup
-        if with_da:
-            acc[rows, :] += dot_nt(dgate, wg_ref[0]) + dot_nt(dup, wu_ref[0])
-
-    for j, (left, right) in enumerate(((at_buf, gu_buf.at[0]), (at_buf, gu_buf.at[1]), (dyt_buf, act_buf))):
-
-        def weights(i, _):
-            rows = pl.ds(pl.multiple_of(i * ROWS, ROWS), ROWS)
-            g_buf[j, rows, :] = dot(left[rows, :], right[...]).astype(BF16)
+        gu_buf[0, rows, :] = (dact * up * (sig + silu * (1 - sig))).astype(BF16)
+        gu_buf[1, rows, :] = (dact * silu).astype(BF16)
+        gu_buf[2, rows, :] = (silu * up).astype(BF16)
+        return 0
+
+    lax.fori_loop(0, steps, hidden, 0)
+
+    def weights(j, _):
+        for i, what in in_weights.items():
+            when((s > 0) & (j == i), functools.partial(due, before, what))
+        g_buf[j] = dot(t_buf[j // 2], gu_buf[j]).astype(BF16)
+        ex.swap(here + j, j).start()
+        when(j > 0, lambda: ex.first(here + j - 1, j - 1))
+        return 0
+
+    lax.fori_loop(0, 3, weights, 0)
+
+    if with_da:
+
+        def by_a(t, _):
+            for i, what in in_da.items():
+                when(t == i, functools.partial(due, here, what))
+            for i, what in before_in_da.items():
+                when((s > 0) & (t == i), functools.partial(due, before, what))
+            rows = chunk(t)
+            acc[rows, :] += dot_nt(gu_buf[0, rows, :], wg_ref[0]) + dot_nt(gu_buf[1, rows, :], wu_ref[0])
             return 0
 
-        lax.fori_loop(0, d // ROWS, weights, 0)
-        ex.swap(3 * s + j, j).start()
-        if j > 0:
-            ex.first(3 * s + j - 1, j - 1)
+        lax.fori_loop(0, steps, by_a, 0)
 
     @pl.when(s == last)
     def _():
-        u = 3 * s
-        ex.first(u + 2, 2)
-        ex.second(u, 0)
         if with_da:
-            dh_ref = refs[2]
-            for rows in chunks:
+
+            def by_h(t, _):
+                rows = chunk(t)
                 wide = h_ref[0, rows, :].astype(F32)
                 scale = norm_scale(wide)
                 da = acc[rows, :].astype(BF16).astype(F32)
-                by_h = da * scale - wide * (scale * scale * scale * jnp.mean(da * wide, -1, keepdims=True))
-                dh_ref[0, rows, :] = dy_ref[0, rows, :] + by_h.astype(BF16)
-        ex.second(u + 1, 1)
-        ex.second(u + 2, 2)
-        for j in range(3):
-            ex.third(u + j, j)
-
-
-def backward(n, layer, with_da, h, dy, weights):
+                through = da * scale - wide * (scale * scale * scale * jnp.mean(da * wide, -1, keepdims=True))
+                dh_ref[0, rows, :] = dy_ref[0, rows, :] + through.astype(BF16)
+                return 0
+
+            lax.fori_loop(0, steps, by_h, 0)
+        due(here, at_last)
+        if with_da:
+            due(before, before_at_last)
+        else:
+            squares_over_group(ex, squares_ref, slots, slot_sems)
+
+
+def backward(n, layer, with_da, h, dy, weights, earlier=()):
     _, tokens, d = h.shape
     ff = weights[0].shape[-1]
     units = 3 * (ff // WIDTH)
     share, chips = d // n, n // 2
-    out_shape = [jax.ShapeDtypeStruct((units, share, WIDTH), BF16), jax.ShapeDtypeStruct((8, 128), F32)]
+    gathered = units - 3 if with_da else 3
+    out_shape = [
+        jax.ShapeDtypeStruct((units, share, WIDTH), BF16),
+        jax.ShapeDtypeStruct((8, 128), F32),
+        jax.ShapeDtypeStruct((gathered, d, WIDTH), BF16),
+    ]
+    out_specs = [once(out_shape[0].shape), once(out_shape[1].shape), pl.BlockSpec(memory_space=pl.ANY)]
     if with_da:
         out_shape.append(jax.ShapeDtypeStruct(h.shape, BF16))
+        out_specs.append(once(h.shape))
+        more = []
+    else:
+        last = units // 3 - 1
+        more = [pl.BlockSpec((3, share, WIDTH), lambda s: (last, 0, 0), pipeline_mode=pl.Buffered(1)), once((8, 128))]
     return pl.pallas_call(
         functools.partial(backward_kernel, n, with_da),
         grid=(ff // WIDTH,),
-        in_specs=[once(h.shape), once(h.shape)] + weight_specs(layer, d),
-        out_specs=[once(o.shape) for o in out_shape],
+        in_specs=[once(h.shape), once(h.shape)] + weight_specs(layer, d) + more,
+        out_specs=out_specs,
         out_shape=out_shape,
         scratch_shapes=[
             pltpu.VMEM((tokens, d), BF16),
-            pltpu.VMEM((d, tokens), BF16),
-            pltpu.VMEM((d, tokens), BF16),
-            pltpu.VMEM((2, tokens, WIDTH), BF16),
-            pltpu.VMEM((tokens, WIDTH), BF16),
+            pltpu.VMEM((2, d, tokens), BF16),
+            pltpu.VMEM((3, tokens, WIDTH), BF16),
             pltpu.VMEM((tokens, d) if with_da else (8, 128), F32),
             pltpu.VMEM((3, d, WIDTH), BF16),
             pltpu.VMEM((units, chips * share, WIDTH), BF16),
             pltpu.VMEM((units, 2, share // 2, WIDTH), BF16),
             pltpu.VMEM((units, 2, share, WIDTH), BF16),
+            pltpu.VMEM((chips + 2, 8, 128), F32),
             pltpu.SemaphoreType.DMA((2, units)),
             pltpu.SemaphoreType.DMA((2, units, 6)),
+            pltpu.SemaphoreType.DMA((2, gathered, 9)),
+            pltpu.SemaphoreType.DMA((gathered,)),
+            pltpu.SemaphoreType.DMA((2, 4)),
         ],
         compiler_params=pltpu.CompilerParams(
             vmem_limit_bytes=VMEM_LIMIT, dimension_semantics=("arbitrary",), collective_id=1 + layer, has_side_effects=True
         ),
         name=f"backward_{layer}",
-    )(h, dy, *weights)
-
-
-def adamw_kernel(f_ref, g_ref, *refs):
+    )(h, dy, *weights, *earlier)
+
+
+def adamw_kernel(count, rows_ref, q_ref, pieces, refs):
     ws, ms, vs = refs[0:3], refs[3:6], refs[6:9]
     new_ws, new_ms, new_vs = refs[9:12], refs[12:15], refs[15:18]
-    factor = f_ref[0]
-    n, _, share, _ = g_ref.shape
+    factor = jnp.minimum(1.0, 0.5 * lax.rsqrt(jnp.full((1, 1), jnp.sum(q_ref[...]) / count, F32) + 1e-30))
 
     def update(g, w, m, v, new_w, new_m, new_v, rows, columns):
         at = (0, rows, columns)
@@ -308,39 +463,80 @@
         new_w[at] = (wide - 0.02 * (m * lax.rsqrt(v + 1e-8) + 0.1 * wide)).astype(BF16)
 
     everything = list(zip(ws, ms, vs, new_ws, new_ms, new_vs, strict=True))
-    place = {i: ((i % 2) * (n // 2) + i // 2) * share for i in range(n)}
+    g_ref = pieces[0]
+    if len(pieces) > 1:
+        g_ref = refs[18]
+        for i, piece in enumerate(pieces):
+            size = piece.shape[1]
+            for j in range(3):
+                g_ref[j, pl.ds(pl.multiple_of(rows_ref[i], size), size), :] = piece[j]
+    d = g_ref.shape[1]
     for j in range(2):
-        for i, row in place.items():
-            update(g_ref[i, j].astype(F32), *everything[j], slice(row, row + share), slice(None))
-    order = sorted(place, key=place.get)
-    half = n // 2
-    for i in range(0, n, half):
-        part = jnp.concatenate([g_ref[k, 2] for k in order[i : i + half]], 0).astype(F32)
-        update(part.T, *everything[2], slice(None), slice(i * share, (i + half) * share))
-
-
-def adamw(factor, layer, g, weights, m, v, earlier):
+        for row in range(0, d, 192):
+            rows = slice(row, row + 192)
+            update(g_ref[j, rows, :].astype(F32), *everything[j], rows, slice(None))
+    for row in range(0, d, 384):
+        rows = slice(row, row + 384)
+        update(g_ref[2, rows, :].astype(F32).T, *everything[2], slice(None), rows)
+
+
+def adamw(squares, layer, slices, pieces, rows, weights, m, v, earlier):
     layers, d, ff = weights[0].shape
-    n, units, share, _ = g.shape
-    wide = pl.BlockSpec((1, d, STRIP), lambda s: (layer, 0, s))
-    tall = pl.BlockSpec((1, STRIP, d), lambda s: (layer, s, 0))
+    strips = WIDTH // STRIP
+    start = slices[0] * strips
+    wide = pl.BlockSpec((1, d, STRIP), lambda s: (layer, 0, start + s))
+    tall = pl.BlockSpec((1, STRIP, d), lambda s: (layer, start + s, 0))
     three = [wide, wide, tall]
-    strips = WIDTH // STRIP
     anywhere = [pl.BlockSpec(memory_space=pl.ANY)] * len(earlier)
-
-    def kernel(f_ref, g_ref, *refs):
-        adamw_kernel(f_ref, g_ref, *refs[:9], *refs[9 + len(earlier) :])
+    count = sum(w.size for w in weights)
+    k, parts = len(pieces), slices[1] - slices[0]
+
+    def kernel(rows_ref, q_ref, *refs):
+        refs = refs[: k + 9] + refs[k + 9 + len(earlier) :]
+        adamw_kernel(count, rows_ref, q_ref, refs[:k], refs[k:])
 
     return pl.pallas_call(
         kernel,
-        grid=(ff // STRIP,),
-        in_specs=[pl.BlockSpec(memory_space=pltpu.SMEM), pl.BlockSpec((n, 3, share, STRIP), lambda s: (0, s // strips, 0, s % strips))] + three * 3 + anywhere,
+        grid=(parts * strips,),
+        in_specs=[pl.BlockSpec(memory_space=pltpu.SMEM), once((8, 128))]
+        + [pl.BlockSpec((3, g.shape[1], STRIP), lambda s: (s // strips, 0, s % strips)) for g in pieces]
+        + three * 3
+        + anywhere,
         out_specs=three * 3,
         out_shape=[jax.ShapeDtypeStruct(w.shape, t) for t in (BF16, F32, F32) for w in weights],
-        input_output_aliases={11 + i: i for i in range(len(earlier))},
+        scratch_shapes=[pltpu.VMEM((3, d, STRIP), BF16)] if k > 1 else [],
+        input_output_aliases={11 + k + i: i for i in range(len(earlier))},
         compiler_params=pltpu.CompilerParams(vmem_limit_bytes=VMEM_LIMIT, dimension_semantics=("arbitrary",)),
-        name=f"adamw_{layer}",
-    )(factor, g, *weights, *m, *v, *earlier)
+        cost_estimate=pl.CostEstimate(flops=10**11 // 6 * parts, bytes_accessed=39 * 10**6 * parts, transcendentals=0),
+        name=f"adamw_{layer}_{slices[0]}",
+    )(rows, squares, *pieces, *weights, *m, *v, *earlier)
+
+
+def gathered(n, own, first, second):
+    chips, share = n // 2, own.shape[1]
+    half = share // 2
+    me = lax.axis_index("dp")
+    core, chip = me % 2, me // 2
+    left, right, far = (chip + chips - 1) % chips, (chip + 1) % chips, (chip + 2) % chips
+
+    def shift(a, by):
+        return lax.ppermute(a, "dp", [(c * 2 + k, (c + by) % chips * 2 + k) for c in range(chips) for k in range(2)])
+
+    def swap(a):
+        return lax.ppermute(a, "dp", [(i, i ^ 1) for i in range(n)])
+
+    from_left, from_right = shift(own, 1), shift(own, -1)
+    result = first()
+    from_left, from_right, result = lax.optimization_barrier((from_left, from_right, result))
+    far_top, far_bottom = shift(from_left[:, :half], 1), shift(from_right[:, half:], -1)
+    near = [own, from_left, from_right]
+    near_there = [swap(piece) for piece in near]
+    result = second(result)
+    far_top, far_bottom, result = lax.optimization_barrier((far_top, far_bottom, result))
+    pieces = near + [far_top, far_bottom] + near_there + [swap(far_top), swap(far_bottom)]
+    rows = [chip * share, left * share, right * share, far * share, far * share + half]
+    rows = [core * chips * share + row for row in rows] + [(1 - core) * chips * share + row for row in rows]
+    return pieces, jnp.stack(rows).astype(jnp.int32), result
 
 
 def solution(mesh):
@@ -348,24 +544,18 @@
 
     def step(x, dy, *arrays):
         weights, m, v = (arrays[i : i + 3] for i in (0, 3, 6))
-        layers = weights[0].shape[0]
-        kept = [x]
-        for number in range(layers - 1):
-            kept.append(forward(number, kept[-1], weights))
-        by_h, own, squares = dy, [None] * layers, []
-        for number in reversed(range(layers)):
-            own[number], part, *rest = backward(n, number, number > 0, kept[number], by_h, weights)
-            squares.append(part)
-            if rest:
-                by_h = rest[0]
-        count = sum(w.size for w in weights)
-        total = lax.psum(sum(jnp.sum(part) for part in squares), "dp")
-        factor = jnp.minimum(1.0, 0.5 * lax.rsqrt(total / count + 1e-30)).reshape(1)
-        new = []
-        for number in reversed(range(layers)):
-            g = lax.all_gather(own[number], "dp")
-            new = adamw(factor, number, g, weights, m, v, new)
-        return tuple(new)
+        slices = weights[0].shape[-1] // WIDTH
+        h = forward(0, x, weights)
+        own_1, squares, g_1, dh = backward(n, 1, True, h, dy, weights)
+        own_0, squares, g_1_last = backward(n, 0, False, x, dh, weights, (own_1, squares))
+        nowhere = jnp.zeros((1,), jnp.int32)
+        pieces, rows, new = gathered(
+            n,
+            own_0,
+            lambda: adamw(squares, 1, (0, slices - 1), [g_1], nowhere, weights, m, v, ()),
+            lambda new: adamw(squares, 1, (slices - 1, slices), [g_1_last], nowhere, weights, m, v, new),
+        )
+        return tuple(adamw(squares, 0, (0, slices), pieces, rows, weights, m, v, new))
 
     return jax.shard_map(
         step,

time: 382 us -> 330 us (0.86); the launches traced: 375 us -> 330 us
  Pallas kernels: 342 us -> 310 us
  between operations: 16.4 us -> 0.91 us
  blocking collectives: 14 us -> 0 us
  waiting for transfers between devices: 0.15 us -> 6.91 us
  starting transfers between devices: 0.13 us -> 6.12 us
  local copies, waits for them, and re-layouts: 0.01 us -> 5.42 us
    pallas_call x2, Pallas kernels: 232 us -> 198 us  [backward(): pl.pallas_call(functools.partial(backward_kernel, n, with_da), grid=(ff /...]
    psum x1 -> x0, blocking collectives: 14 us -> none  [step(): total = lax.psum(sum((jnp.sum(part) for part in squares)), 'dp')]
    ppermute x0 -> x9, waiting for transfers between devices: none -> 6.91 us  [the longest x4 4.84 us: shift(): lax.ppermute(a, 'dp', [(c * 2 + k, (c + by) % chips * 2 + k) for c in ran...]
    ppermute x0 -> x9, starting transfers between devices: none -> 6.12 us  [the longest x5 3.18 us: swap(): return lax.ppermute(a, 'dp', [(i, i ^ 1) for i in range(n)])]
    slice x0 -> x2, local copies, waits for them, and re-layouts: none -> 3.96 us  [the longest x1 1.98 us: gathered(): from_right[:, half:]]
    pallas_call x2 -> x3, Pallas kernels: 80.5 us -> 82.7 us  [adamw(): pl.pallas_call(kernel, grid=(parts * strips,), in_specs=[pl.BlockSpec(mem...]
  transfers between devices with their start and end apart: 2 -> 9, of which waited for: 0 -> 4; matrix products, arithmetic and copies ran while one was open for 1% -> 1% of each run, Pallas kernels for 40% -> 13%
where the time goes in v3:
time: 330 us
  Pallas kernels  310 us (94%)
  waiting for transfers between devices  6.91 us (2%)
  starting transfers between devices  6.12 us (2%)
  local copies, waits for them, and re-layouts  5.42 us (2%)
    pallas_call x2, Pallas kernels, backward(): pl.pallas_call(functools.partial(backward_kernel, n, with_da), grid=(ff /...  198 us
    pallas_call x3, Pallas kernels, adamw(): pl.pallas_call(kernel, grid=(parts * strips,), in_specs=[pl.BlockSpec(mem...  82.7 us
    pallas_call x1, Pallas kernels, forward(): pl.pallas_call(forward_kernel, grid=(ff // WIDTH,), in_specs=[once(h.shap...  29.8 us
  transfers between devices with their start and end apart: 9, of which 4 were waited for; matrix products, arithmetic and copies ran while one was open for 1% of the time, Pallas kernels for 13%

profile of v3, /device:TPU:113, one launch (start us, length us, event | category | flops | bytes accessed | tf_op | source)
XLA Modules:
  0.0 329.7 jit_solution(13655332687910152942)
XLA Ops:
  0.6 29.8 %forward.1.h_ref = bf16[1,2048,768]{2,1,0:T(8,128)(2,1)} custom-call(bf16[1,2048,768]{2,1,0:T(8,128)(2,1)} %h_ref.3, bf16[2,768,2304]{2,1,0:T(8,128)(2,1)} %refs_10_.1, bf16[2,768,2304]{2,1,0:T(8,128)(2,1)} %refs_11_.1, bf16[2,2304,768]{2,1,0:T(8,128)(2,1)} %refs_12_.1), custom_call_target="tpu_custom_call" | custom-call | tf_op jit(solution)/shard_map/forward/pallas_call | solution.py:73
  30.4 105.5 %backward_1.1 = (bf16[9,96,768]{2,1,0:T(8,128)(2,1)}, f32[8,128]{1,0:T(8,128)}, bf16[6,768,768]{2,1,0:T(8,128)(2,1)}, bf16[1,2048,768]{2,1,0:T(8,128)(2,1)}) custom-call(bf16[1,2048,768]{2,1,0:T(8,128)(2,1)} %forward.1.h_ref, bf16[1,2048,768]{2,1,0:T(8,128)(2,1)} %dy_ref.1, bf16[2,768,2304]{2,1,0:T(8,128)(2,1)} %refs_10_.1, bf16[2,768,2304]{2,1,0:T(8,128)(2,1)} %refs_11_.1, ...), custom_call_target="tpu_custom_call" | custom-call | tf_op jit(solution)/shard_map/backward_1/pallas_call | solution.py:421
  135.9 92.4 %backward_0.1 = (bf16[9,96,768]{2,1,0:T(8,128)(2,1)}, f32[8,128]{1,0:T(8,128)}, bf16[3,768,768]{2,1,0:T(8,128)(2,1)}) custom-call(bf16[1,2048,768]{2,1,0:T(8,128)(2,1)} %h_ref.3, bf16[1,2048,768]{2,1,0:T(8,128)(2,1)} %get-tuple-element.56.dy_ref, bf16[2,768,2304]{2,1,0:T(8,128)(2,1)} %refs_10_.1, bf16[2,768,2304]{2,1,0:T(8,128)(2,1)} %refs_11_.1, ...), custom_call_target="tpu_custom_call" | custom-call | tf_op jit(solution)/shard_map/backward_0/pallas_call | solution.py:421
  228.4 0.8 collective-permute-start.4
  229.2 1.2 collective-permute-start.1
  230.3 0.3 collective-permute-start
  230.6 26.5 %adamw_1_0.1 = (bf16[2,768,2304]{2,1,0:T(8,128)(2,1)}, bf16[2,768,2304]{2,1,0:T(8,128)(2,1)}, bf16[2,2304,768]{2,1,0:T(8,128)(2,1)}, f32[2,768,2304]{2,1,0:T(8,1...) custom-call(s32[1]{0:T(128)} %constant.57.clone.1.rows_ref, ...), custom_call_target="tpu_custom_call" | custom-call | flops 33333334016 | bytes 78000000 | tf_op jit(solution)/shard_map/adamw_1_0/pallas_call | solution.py:498
  257.1 2.7 collective-permute-done.1.refs_2_
  259.9 2.1 collective-permute-done.refs_1_
  262.0 2.0 slice.6
  263.9 1.1 collective-permute-start.5
  265.1 2.0 slice.7
  267.1 0.0 collective-permute-start.6
  267.1 0.0 collective-permute-start.3
  267.1 1.5 collective-permute-start.2
  268.5 15.8 %adamw_1_2.1 = (bf16[2,768,2304]{2,1,0:T(8,128)(2,1)}, bf16[2,768,2304]{2,1,0:T(8,128)(2,1)}, bf16[2,2304,768]{2,1,0:T(8,128)(2,1)}, f32[2,768,2304]{2,1,0:T(8,1...) custom-call(s32[1]{0:T(128)} %constant.57.clone.1.rows_ref, ...), custom_call_target="tpu_custom_call", output_to_operand_aliasing={{0}: (12, {}), {1}: (13, {}), {2}: (14, {}), {3}: (15, {}),... | custom-call | flops 16666667008 | bytes 39000000 | tf_op jit(solution)/shard_map/adamw_1_2/pallas_call | solution.py:498
  284.3 0.0 collective-permute-done.3.refs_4_
  284.4 0.0 copy-start
  284.4 0.0 collective-permute-done.2.refs_3_
  284.4 1.2 collective-permute-start.7
  285.6 0.0 collective-permute-start.8
  285.6 0.6 stack.43.rows_ref
  286.2 0.0 collective-permute-done.4.refs_5_
  286.2 1.1 collective-permute-done.7.refs_8_
  287.3 0.0 copy-start.1
  287.3 0.9 collective-permute-done.8.refs_9_
  288.3 0.0 copy-done.1
  288.3 0.0 copy-start.2
  288.3 0.0 collective-permute-done.5.refs_6_
  288.3 0.8 copy-done.2
  289.1 0.0 collective-permute-done.6.refs_7_
  289.1 0.0 copy-done
  289.2 40.4 %adamw_0_0.1 = (bf16[2,768,2304]{2,1,0:T(8,128)(2,1)}, bf16[2,768,2304]{2,1,0:T(8,128)(2,1)}, bf16[2,2304,768]{2,1,0:T(8,128)(2,1)}, f32[2,768,2304]{2,1,0:T(8,1...) custom-call(s32[10]{0:T(128)} %stack.43.rows_ref, ...), custom_call_target="tpu_custom_call", output_to_operand_aliasing={{0}: (21, {}), {1}: (22, {}), {2}: (23, {}), {3}: (24, {}),... | custom-call | flops 49999998976 | bytes 117000000 | tf_op jit(solution)/shard_map/adamw_0_0/pallas_call | solution.py:498
Async XLA Ops:
  228.4 57.9 %collective-permute-start.4 = (bf16[9,96,768]{2,1,0:T(8,128)(2,1)}, bf16[9,96,768]{2,1,0:T(8,128)(2,1)}, u32[]{:S(2)}, u32[]{:S(2)}) collective-permute-start(bf16[9,96,768]{2,1,0:T(8,128)(2,1)} %get-tuple-element.60.refs_0_), channel_id=1, source_target_pairs={{0,1},{1,0},{2,3},{3,2},{4,5},{5,4},{6,7},{7,6},{8,9},{9,8},{10,11... | collective-permute-start | bytes 3981320 | tf_op jit(solution)/shard_map/ppermute | solution.py:526
  229.2 30.7 %collective-permute-start.1 = (bf16[9,96,768]{2,1,0:T(8,128)(2,1)}, bf16[9,96,768]{2,1,0:T(8,128)(2,1)}, u32[]{:S(2)}, u32[]{:S(2)}) collective-permute-start(bf16[9,96,768]{2,1,0:T(8,128)(2,1)} %get-tuple-element.60.refs_0_), channel_id=1, source_target_pairs={{0,6},{1,7},{2,0},{3,1},{4,2},{5,3},{6,4},{7,5},{8,14},{9,15},{10,... | collective-permute-start | bytes 3981320 | tf_op jit(solution)/shard_map/ppermute | solution.py:523
  230.3 31.6 %collective-permute-start = (bf16[9,96,768]{2,1,0:T(8,128)(2,1)}, bf16[9,96,768]{2,1,0:T(8,128)(2,1)}, u32[]{:S(2)}, u32[]{:S(2)}) collective-permute-start(bf16[9,96,768]{2,1,0:T(8,128)(2,1)} %get-tuple-element.60.refs_0_), channel_id=1, source_target_pairs={{0,2},{1,3},{2,4},{3,5},{4,6},{5,7},{6,0},{7,1},{8,10},{9,11},{10,... | collective-permute-start | bytes 3981320 | tf_op jit(solution)/shard_map/ppermute | solution.py:523
  263.9 24.4 %collective-permute-start.5 = (bf16[9,96,768]{2,1,0:T(8,128)(2,1)}, bf16[9,96,768]{2,1,0:T(8,128)(2,1)}, u32[]{:S(2)}, u32[]{:S(2)}) collective-permute-start(bf16[9,96,768]{2,1,0:T(8,128)(2,1)} %collective-permute-done.refs_1_), channel_id=1, source_target_pairs={{0,1},{1,0},{2,3},{3,2},{4,5},{5,4},{6,7},{7,6},{8,9},{9,8},{10,11... | collective-permute-start | bytes 3981320 | tf_op jit(solution)/shard_map/ppermute | solution.py:526
  267.1 22.1 %collective-permute-start.6 = (bf16[9,96,768]{2,1,0:T(8,128)(2,1)}, bf16[9,96,768]{2,1,0:T(8,128)(2,1)}, u32[]{:S(2)}, u32[]{:S(2)}) collective-permute-start(bf16[9,96,768]{2,1,0:T(8,128)(2,1)} %collective-permute-done.1.refs_2_), channel_id=1, source_target_pairs={{0,1},{1,0},{2,3},{3,2},{4,5},{5,4},{6,7},{7,6},{8,9},{9,8},{10,11... | collective-permute-start | bytes 3981320 | tf_op jit(solution)/shard_map/ppermute | solution.py:526
  267.1 17.3 %collective-permute-start.3 = (bf16[9,48,768]{2,1,0:T(8,128)(2,1)}, bf16[9,48,768]{2,1,0:T(8,128)(2,1)S(1)}, u32[]{:S(2)}, u32[]{:S(2)}) collective-permute-start(bf16[9,48,768]{2,1,0:T(8,128)(2,1)} %slice.7), channel_id=1, source_target_pairs={{0,6},{1,7},{2,0},{3,1},{4,2},{5,3},{6,4},{7,5},{8,14},{9,15},{10,... | collective-permute-start | bytes 1990664 | tf_op jit(solution)/shard_map/ppermute | solution.py:523
  267.1 17.3 %collective-permute-start.2 = (bf16[9,48,768]{2,1,0:T(8,128)(2,1)}, bf16[9,48,768]{2,1,0:T(8,128)(2,1)}, u32[]{:S(2)}, u32[]{:S(2)}) collective-permute-start(bf16[9,48,768]{2,1,0:T(8,128)(2,1)} %slice.6), channel_id=1, source_target_pairs={{0,2},{1,3},{2,4},{3,5},{4,6},{5,7},{6,0},{7,1},{8,10},{9,11},{10,... | collective-permute-start | bytes 1990664 | tf_op jit(solution)/shard_map/ppermute | solution.py:523
  284.4 4.8 %copy-start = (bf16[9,48,768]{2,1,0:T(8,128)(2,1)}, bf16[9,48,768]{2,1,0:T(8,128)(2,1)S(1)}, u32[]{:S(2)}) copy-start(bf16[9,48,768]{2,1,0:T(8,128)(2,1)S(1)} %collective-permute-done.3.refs_4_) | copy-start | bytes 1990660
  284.4 3.0 collective-permute-start.7
  285.6 2.7 collective-permute-start.8
  287.3 1.0 copy-start.1
  288.3 0.8 copy-start.2

commit v4 on v3

--- a/solution.py
+++ b/solution.py
@@ -12,7 +12,7 @@
 WIDTH = 768
 STRIP = 256
 CHUNK = 512
-ROWS = 256
+SLOTS = 6
 VMEM_LIMIT = 63 * 1024 * 1024
 NT = (((1,), (1,)), ((), ()))
 
@@ -38,28 +38,62 @@
     return pl.BlockSpec(shape, lambda *_: (0,) * len(shape), pipeline_mode=pl.Buffered(1))
 
 
-def forward_kernel(h_ref, wg_ref, wu_ref, wd_ref, out_ref, a_buf, acc):
+def forward_kernel(h_ref, wg_ref, wu_ref, wd_ref, out_ref, gate_hbm, up_hbm, a_buf, acc, stage, sems):
     s = pl.program_id(0)
     tokens = a_buf.shape[0]
-    chunks = [pl.ds(t, CHUNK) for t in range(0, tokens, CHUNK)]
+    steps = tokens // CHUNK
+    count = pl.num_programs(0) * steps
+
+    def chunk(t):
+        return pl.ds(pl.multiple_of(t * CHUNK, CHUNK), CHUNK)
+
+    def keep(step):
+        slot = lax.rem(step, 2)
+        return [pltpu.make_async_copy(stage.at[slot, i], to.at[step // steps, chunk(lax.rem(step, steps))], sems.at[slot, i]) for i, to in enumerate((gate_hbm, up_hbm))]
 
     @pl.when(s == 0)
     def _():
-        for rows in chunks:
+        def prepare(t, _):
+            rows = chunk(t)
             a_buf[rows, :] = normed(h_ref[0, rows, :])
             acc[rows, :] = jnp.zeros((CHUNK, acc.shape[1]), F32)
-
-    for rows in chunks:
+            return 0
+
+        lax.fori_loop(0, steps, prepare, 0)
+
+    def hidden(t, _):
+        rows, step = chunk(t), s * steps + t
+        slot = lax.rem(step, 2)
+
+        @pl.when(step >= 2)
+        def _():
+            for copy in keep(step - 2):
+                copy.wait()
+
         a = a_buf[rows, :]
         gate = dot(a, wg_ref[0])
         up = dot(a, wu_ref[0])
+        stage[slot, 0] = gate
+        stage[slot, 1] = up
+        for copy in keep(step):
+            copy.start()
         act = (gate * jax.nn.sigmoid(gate) * up).astype(BF16)
         acc[rows, :] += dot(act, wd_ref[0])
+        return 0
+
+    lax.fori_loop(0, steps, hidden, 0)
 
     @pl.when(s == pl.num_programs(0) - 1)
     def _():
-        for rows in chunks:
+        def finish(t, _):
+            rows = chunk(t)
             out_ref[0, rows, :] = h_ref[0, rows, :] + acc[rows, :].astype(BF16)
+            return 0
+
+        lax.fori_loop(0, steps, finish, 0)
+        for step in (count - 2, count - 1):
+            for copy in keep(step):
+                copy.wait()
 
 
 def weight_specs(layer, d):
@@ -70,22 +104,28 @@
 def forward(layer, h, weights):
     _, tokens, d = h.shape
     ff = weights[0].shape[-1]
+    kept = jax.ShapeDtypeStruct((ff // WIDTH, tokens, WIDTH), F32)
     return pl.pallas_call(
         forward_kernel,
         grid=(ff // WIDTH,),
         in_specs=[once(h.shape)] + weight_specs(layer, d),
-        out_specs=once(h.shape),
-        out_shape=jax.ShapeDtypeStruct(h.shape, BF16),
-        scratch_shapes=[pltpu.VMEM((tokens, d), BF16), pltpu.VMEM((tokens, d), F32)],
+        out_specs=[once(h.shape), pl.BlockSpec(memory_space=pl.ANY), pl.BlockSpec(memory_space=pl.ANY)],
+        out_shape=[jax.ShapeDtypeStruct(h.shape, BF16), kept, kept],
+        scratch_shapes=[
+            pltpu.VMEM((tokens, d), BF16),
+            pltpu.VMEM((tokens, d), F32),
+            pltpu.VMEM((2, 2, CHUNK, WIDTH), F32),
+            pltpu.SemaphoreType.DMA((2, 2)),
+        ],
         compiler_params=pltpu.CompilerParams(vmem_limit_bytes=VMEM_LIMIT, dimension_semantics=("arbitrary",)),
         name="forward",
     )(h, *weights)
 
 
 class Exchange:
-    def __init__(self, n, g_buf, got_half, got_far, got_near, own_ref, squares, sems):
+    def __init__(self, n, g_buf, got_half, got_far, got_near, own_refs, squares, sems):
         self.g_buf, self.got_half, self.got_far, self.got_near = g_buf, got_half, got_far, got_near
-        self.own_ref, self.squares = own_ref, squares
+        self.own_refs, self.squares = own_refs, squares
         self.swap_sems, self.sems = sems
         me = lax.axis_index("dp")
         self.core, self.chip = lax.rem(me, 2), me // 2
@@ -164,7 +204,11 @@
             self.copy(u, slot, which).wait_recv()
         total = self.at(slot, self.chip)[...].astype(F32) + self.got_near[u, 0].astype(F32) + self.got_near[u, 1].astype(F32)
         total = total.astype(BF16)
-        self.own_ref[u] = total
+        if len(self.own_refs) == 1:
+            self.own_refs[0][u] = total
+        else:
+            for part, half in zip(self.own_refs, (total[: self.share // 2], total[self.share // 2 :]), strict=True):
+                part[u] = half
         wide = total.astype(F32)
         wide = (wide * wide).reshape(-1, 8, wide.shape[-1]).sum(0)
         self.squares[...] += sum(wide[:, i : i + 128] for i in range(0, wide.shape[-1], 128))
@@ -260,18 +304,21 @@
     squares_ref[...] = total
 
 
-def backward_kernel(n, with_da, h_ref, dy_ref, wg_ref, wu_ref, wd_ref, *refs):
+def backward_kernel(n, with_da, h_ref, dy_ref, *refs):
     if with_da:
-        own_ref, squares_ref, gathered_ref, dh_ref, *refs = refs
+        wg_ref, wu_ref, wd_ref, squares_ref, gathered_ref, own_ref, dh_ref, a_buf, acc, *refs = refs
+        own_refs = (own_ref,)
     else:
-        earlier_own_ref, earlier_squares_ref, own_ref, squares_ref, gathered_ref, *refs = refs
-    a_buf, t_buf, gu_buf, acc, g_buf, got_half, got_far, got_near, slots, *sems = refs
+        wd_ref, gate_hbm, up_hbm, earlier_own_ref, earlier_squares_ref, squares_ref, gathered_ref, *own_refs, stage, stage_sems = refs[:11]
+        refs = refs[11:]
+    t_buf, gu_buf, g_buf, got_half, got_far, got_near, slots, *sems = refs
     swap_sems, copy_sems, gather_sems, local_sems, slot_sems = sems
+    depth = g_buf.shape[0]
     s = pl.program_id(0)
     last = pl.num_programs(0) - 1
-    tokens, d = a_buf.shape
+    _, tokens, d = h_ref.shape
     steps = tokens // CHUNK
-    ex = Exchange(n, g_buf, got_half, got_far, got_near, own_ref, squares_ref, (swap_sems, copy_sems))
+    ex = Exchange(n, g_buf, got_half, got_far, got_near, own_refs, squares_ref, (swap_sems, copy_sems))
     gather = Gather(ex, own_ref if with_da else earlier_own_ref, 0, gathered_ref, gather_sems, local_sems)
 
     def chunk(t):
@@ -280,8 +327,15 @@
     def each(f, start=0):
         lax.fori_loop(0, 3, lambda j, _: (f(start + j), 0)[1], 0)
 
+    def fetch(step):
+        slot = lax.rem(step, 2)
+        return [pltpu.make_async_copy(kept.at[step // steps, chunk(lax.rem(step, steps))], stage.at[slot, i], stage_sems.at[slot, i]) for i, kept in enumerate((gate_hbm, up_hbm))]
+
     @pl.when(s == 0)
     def _():
+        if not with_da:
+            for copy in fetch(0):
+                copy.start()
         ex.barrier(not with_da)
         if with_da:
             squares_ref[...] = jnp.zeros_like(squares_ref)
@@ -292,10 +346,10 @@
         def prepare(t, _):
             rows = chunk(t)
             a = normed(h_ref[0, rows, :])
-            a_buf[rows, :] = a
             t_buf[0, :, rows] = a.T
             t_buf[1, :, rows] = dy_ref[0, rows, :].T
             if with_da:
+                a_buf[rows, :] = a
                 acc[rows, :] = jnp.zeros((CHUNK, d), F32)
             return 0
 
@@ -306,7 +360,7 @@
         gathers = {"1": gather.one, "2": gather.two, "3": gather.three, "4": gather.four}
         for step, j in zip(what[::2], map(int, what[1::2])):
             if step in steps:
-                steps[step](u + j, j)
+                steps[step](u + j, lax.rem(u + j, depth))
             else:
                 gathers[step](u + j)
 
@@ -319,17 +373,15 @@
                 action()
 
     if with_da:
-        in_hidden = {0: "s1", 1: "s2", 2: "t010", 3: "t111"}
-        in_weights = {0: "t212", 1: "20", 2: "21"}
-        in_da = {1: "f2", 2: "s0"}
-        before_in_da = {0: "2230", 2: "31"}
-        earlier_in_hidden = {0: "32", 3: "404142"}
-        at_last, before_at_last = "s1s2t0t1t2", "32404142"
+        in_hidden = {1: "s2", 2: "t010t111", 3: "t212"}
+        in_weights = {0: "20", 1: "21", 2: "22"}
+        in_da = {1: "f2", 2: "s0", 3: "s1"}
+        before_in_da = {0: "30", 1: "31", 3: "32"}
+        earlier_in_hidden = {0: "404142"}
     else:
-        in_hidden = {1: "f2s0", 2: "s1"}
-        in_weights = {0: "s2t0", 1: "t1", 2: "t2"}
-        earlier_in_hidden = {}
-        at_last = "s0f2s1t0s2t1t2"
+        in_hidden = {1: "f2", 2: "s0"}
+        in_weights = {0: "s1", 1: "s2", 2: "t0"}
+        earlier_in_hidden = {0: "t1", 2: "t2"}
 
     def hidden(t, _):
         for i, what in in_hidden.items():
@@ -337,14 +389,20 @@
         for i, what in earlier_in_hidden.items():
             when((s > 1) & (t == i), functools.partial(due, before - 3, what))
         if not with_da:
-            when((s == 0) & (t == 1), functools.partial(due, 0, "20"))
-            when((s == 0) & (t == 2), functools.partial(due, 0, "21"))
-            when((s == 0) & (t == 3), functools.partial(due, 0, "2230"))
-            when((s == 1) & (t == 0), functools.partial(due, 0, "3132404142"))
+            when((s == 0) & (t == 3), functools.partial(due, 0, "20"))
+            when((s == 1) & (t == 0), functools.partial(due, 0, "31"))
+            when((s == 1) & (t == 2), functools.partial(due, 0, "32"))
         rows = chunk(t)
-        a = a_buf[rows, :]
-        gate = dot(a, wg_ref[0])
-        up = dot(a, wu_ref[0])
+        if with_da:
+            a = a_buf[rows, :]
+            gate = dot(a, wg_ref[0])
+            up = dot(a, wu_ref[0])
+        else:
+            step = s * steps + t
+            for copy in fetch(step):
+                copy.wait()
+            when(step + 1 < pl.num_programs(0) * steps, lambda: [copy.start() for copy in fetch(step + 1)])
+            gate, up = stage[lax.rem(step, 2), 0], stage[lax.rem(step, 2), 1]
         dact = dot_nt(dy_ref[0, rows, :], wd_ref[0]).astype(BF16).astype(F32)
         sig = jax.nn.sigmoid(gate)
         silu = gate * sig
@@ -358,9 +416,14 @@
     def weights(j, _):
         for i, what in in_weights.items():
             when((s > 0) & (j == i), functools.partial(due, before, what))
-        g_buf[j] = dot(t_buf[j // 2], gu_buf[j]).astype(BF16)
-        ex.swap(here + j, j).start()
-        when(j > 0, lambda: ex.first(here + j - 1, j - 1))
+        if not with_da:
+            when((s == 0) & (j == 1), functools.partial(due, 0, "21"))
+            when((s == 0) & (j == 2), functools.partial(due, 0, "2230"))
+            when((s == 1) & (j == 0), functools.partial(due, 0, "404142"))
+        slot = lax.rem(here + j, depth)
+        g_buf[slot] = dot(t_buf[j // 2], gu_buf[j]).astype(BF16)
+        ex.swap(here + j, slot).start()
+        when(j > 0, lambda: ex.first(here + j - 1, lax.rem(here + j - 1, depth)))
         return 0
 
     lax.fori_loop(0, 3, weights, 0)
@@ -392,10 +455,14 @@
                 return 0
 
             lax.fori_loop(0, steps, by_h, 0)
-        due(here, at_last)
         if with_da:
-            due(before, before_at_last)
+            due(before, "404142")
+            due(here, "s2t0t1t2")
         else:
+            due(before, "t1")
+            due(here, "s0f2")
+            due(before, "t2")
+            due(here, "s1t0s2t1t2")
             squares_over_group(ex, squares_ref, slots, slot_sems)
 
 
@@ -406,30 +473,34 @@
     share, chips = d // n, n // 2
     gathered = units - 3 if with_da else 3
     out_shape = [
-        jax.ShapeDtypeStruct((units, share, WIDTH), BF16),
         jax.ShapeDtypeStruct((8, 128), F32),
         jax.ShapeDtypeStruct((gathered, d, WIDTH), BF16),
     ]
-    out_specs = [once(out_shape[0].shape), once(out_shape[1].shape), pl.BlockSpec(memory_space=pl.ANY)]
+    out_specs = [once(out_shape[0].shape), pl.BlockSpec(memory_space=pl.ANY)]
     if with_da:
-        out_shape.append(jax.ShapeDtypeStruct(h.shape, BF16))
-        out_specs.append(once(h.shape))
-        more = []
+        out_shape += [jax.ShapeDtypeStruct((units, share, WIDTH), BF16), jax.ShapeDtypeStruct(h.shape, BF16)]
+        more = weight_specs(layer, d)
+        scratch = [pltpu.VMEM((tokens, d), BF16), pltpu.VMEM((tokens, d), F32)]
     else:
+        out_shape += [jax.ShapeDtypeStruct((units, share // 2, WIDTH), BF16)] * 2
         last = units // 3 - 1
-        more = [pl.BlockSpec((3, share, WIDTH), lambda s: (last, 0, 0), pipeline_mode=pl.Buffered(1)), once((8, 128))]
+        anywhere = pl.BlockSpec(memory_space=pl.ANY)
+        share_spec = pl.BlockSpec((3, share, WIDTH), lambda s: (last, 0, 0), pipeline_mode=pl.Buffered(1))
+        more = weight_specs(layer, d)[2:] + [anywhere, anywhere, share_spec, once((8, 128))]
+        weights = weights[2:]
+        scratch = [pltpu.VMEM((2, 2, CHUNK, WIDTH), F32), pltpu.SemaphoreType.DMA((2, 2))]
+    out_specs += [once(o.shape) for o in out_shape[2:]]
     return pl.pallas_call(
         functools.partial(backward_kernel, n, with_da),
         grid=(ff // WIDTH,),
-        in_specs=[once(h.shape), once(h.shape)] + weight_specs(layer, d) + more,
+        in_specs=[once(h.shape), once(h.shape)] + more,
         out_specs=out_specs,
         out_shape=out_shape,
-        scratch_shapes=[
-            pltpu.VMEM((tokens, d), BF16),
+        scratch_shapes=scratch
+        + [
             pltpu.VMEM((2, d, tokens), BF16),
             pltpu.VMEM((3, tokens, WIDTH), BF16),
-            pltpu.VMEM((tokens, d) if with_da else (8, 128), F32),
-            pltpu.VMEM((3, d, WIDTH), BF16),
+            pltpu.VMEM((SLOTS, d, WIDTH), BF16),
             pltpu.VMEM((units, chips * share, WIDTH), BF16),
             pltpu.VMEM((units, 2, share // 2, WIDTH), BF16),
             pltpu.VMEM((units, 2, share, WIDTH), BF16),
@@ -513,8 +584,8 @@
 
 
 def gathered(n, own, first, second):
-    chips, share = n // 2, own.shape[1]
-    half = share // 2
+    chips, half = n // 2, own[0].shape[1]
+    share = 2 * half
     me = lax.axis_index("dp")
     core, chip = me % 2, me // 2
     left, right, far = (chip + chips - 1) % chips, (chip + 1) % chips, (chip + 2) % chips
@@ -525,16 +596,18 @@
     def swap(a):
         return lax.ppermute(a, "dp", [(i, i ^ 1) for i in range(n)])
 
-    from_left, from_right = shift(own, 1), shift(own, -1)
+    top, bottom = own
+    from_left = [shift(top, 1), shift(bottom, 1)]
+    from_right = [shift(bottom, -1), shift(top, -1)]
     result = first()
     from_left, from_right, result = lax.optimization_barrier((from_left, from_right, result))
-    far_top, far_bottom = shift(from_left[:, :half], 1), shift(from_right[:, half:], -1)
-    near = [own, from_left, from_right]
+    far_top, far_bottom = shift(from_left[0], 1), shift(from_right[0], -1)
+    near = [top, bottom, *from_left, *from_right]
     near_there = [swap(piece) for piece in near]
     result = second(result)
     far_top, far_bottom, result = lax.optimization_barrier((far_top, far_bottom, result))
     pieces = near + [far_top, far_bottom] + near_there + [swap(far_top), swap(far_bottom)]
-    rows = [chip * share, left * share, right * share, far * share, far * share + half]
+    rows = [chip * share, chip * share + half, left * share, left * share + half, right * share + half, right * share, far * share, far * share + half]
     rows = [core * chips * share + row for row in rows] + [(1 - core) * chips * share + row for row in rows]
     return pieces, jnp.stack(rows).astype(jnp.int32), result
 
@@ -545,9 +618,9 @@
     def step(x, dy, *arrays):
         weights, m, v = (arrays[i : i + 3] for i in (0, 3, 6))
         slices = weights[0].shape[-1] // WIDTH
-        h = forward(0, x, weights)
-        own_1, squares, g_1, dh = backward(n, 1, True, h, dy, weights)
-        own_0, squares, g_1_last = backward(n, 0, False, x, dh, weights, (own_1, squares))
+        h, gate, up = forward(0, x, weights)
+        squares, g_1, own_1, dh = backward(n, 1, True, h, dy, weights)
+        squares, g_1_last, *own_0 = backward(n, 0, False, x, dh, weights, (gate, up, own_1, squares))
         nowhere = jnp.zeros((1,), jnp.int32)
         pieces, rows, new = gathered(
             n,

time: 330 us -> 316 us (0.958)
  Pallas kernels: 310 us -> 297 us
  starting transfers between devices: 6.12 us -> 11.3 us
  local copies, waits for them, and re-layouts: 5.42 us -> 0.67 us
    pallas_call x2, Pallas kernels: 198 us -> 182 us  [backward(): pl.pallas_call(functools.partial(backward_kernel, n, with_da), grid=(ff /...]
    slice x2 -> x0, local copies, waits for them, and re-layouts: 3.96 us -> none  [the longest x1 1.98 us: gathered(): from_right[:, half:]]
    ppermute x4 -> x6, starting transfers between devices: 2.93 us -> 6.66 us  [shift(): lax.ppermute(a, 'dp', [(c * 2 + k, (c + by) % chips * 2 + k) for c in ran...]
    pallas_call x1, Pallas kernels: 29.8 us -> 33.3 us  [forward(): pl.pallas_call(forward_kernel, grid=(ff // WIDTH,), in_specs=[once(h.shap...]
    ppermute x4 -> x6, waiting for transfers between devices: 4.84 us -> 1.37 us  [shift(): lax.ppermute(a, 'dp', [(c * 2 + k, (c + by) % chips * 2 + k) for c in ran...]
  transfers between devices with their start and end apart: 9 -> 14, of which waited for: 4 -> 4; matrix products, arithmetic and copies ran while one was open for 1% -> 0% of each run, Pallas kernels for 13% -> 13%
where the time goes in v4:
time: 316 us; the launch traced here: 315 us
  Pallas kernels  297 us (94%)
  starting transfers between devices  11.3 us (4%)
  waiting for transfers between devices  5.21 us (2%)
    pallas_call x2, Pallas kernels, backward(): pl.pallas_call(functools.partial(backward_kernel, n, with_da), grid=(ff /...  182 us
    pallas_call x3, Pallas kernels, adamw(): pl.pallas_call(kernel, grid=(parts * strips,), in_specs=[pl.BlockSpec(mem...  82.5 us
    pallas_call x1, Pallas kernels, forward(): pl.pallas_call(forward_kernel, grid=(ff // WIDTH,), in_specs=[once(h.shap...  33.3 us
    ppermute x6, starting transfers between devices, shift(): lax.ppermute(a, 'dp', [(c * 2 + k, (c + by) % chips * 2 + k) for c in ran...  6.66 us
  transfers between devices with their start and end apart: 14, of which 4 were waited for; matrix products, arithmetic and copies ran while one was open for 0% of the time, Pallas kernels for 13%

profile of v4, /device:TPU:113, one launch (start us, length us, event | category | flops | bytes accessed | tf_op | source)
XLA Modules:
  0.0 315.4 jit_solution(2411167555415427431)
XLA Ops:
  0.6 33.3 %forward.1 = (bf16[1,2048,768]{2,1,0:T(8,128)(2,1)}, f32[3,2048,768]{2,1,0:T(8,128)}, f32[3,2048,768]{2,1,0:T(8,128)}) custom-call(bf16[1,2048,768]{2,1,0:T(8,128)(2,1)} %h_ref.3, bf16[2,768,2304]{2,1,0:T(8,128)(2,1)} %refs_16_.1, bf16[2,768,2304]{2,1,0:T(8,128)(2,1)} %refs_17_.1, bf16[2,2304,768]{2,1,0:T(8,128)(2,1)} %refs_18_.1), custom_call_target="tpu_custom_call" | custom-call | tf_op jit(solution)/shard_map/forward/pallas_call | solution.py:108
  33.9 103.6 %backward_1.1 = (f32[8,128]{1,0:T(8,128)}, bf16[6,768,768]{2,1,0:T(8,128)(2,1)}, bf16[9,96,768]{2,1,0:T(8,128)(2,1)}, bf16[1,2048,768]{2,1,0:T(8,128)(2,1)}) custom-call(bf16[1,2048,768]{2,1,0:T(8,128)(2,1)} %get-tuple-element.62.h_ref, bf16[1,2048,768]{2,1,0:T(8,128)(2,1)} %dy_ref.1, bf16[2,768,2304]{2,1,0:T(8,128)(2,1)} %refs_16_.1, ...), custom_call_target="tpu_custom_call" | custom-call | tf_op jit(solution)/shard_map/backward_1/pallas_call | solution.py:493
  137.5 77.9 %backward_0.1 = (f32[8,128]{1,0:T(8,128)}, bf16[3,768,768]{2,1,0:T(8,128)(2,1)}, bf16[9,48,768]{2,1,0:T(8,128)(2,1)}, bf16[9,48,768]{2,1,0:T(8,128)(2,1)}) custom-call(bf16[1,2048,768]{2,1,0:T(8,128)(2,1)} %h_ref.3, bf16[1,2048,768]{2,1,0:T(8,128)(2,1)} %get-tuple-element.63.dy_ref, bf16[2,2304,768]{2,1,0:T(8,128)(2,1)} %refs_18_.1, ...), custom_call_target="tpu_custom_call" | custom-call | tf_op jit(solution)/shard_map/backward_0/pallas_call | solution.py:493
  215.5 0.8 collective-permute-start.6
  216.3 1.3 collective-permute-start.3
  217.6 0.2 collective-permute-start
  217.8 2.5 collective-permute-start.2
  220.3 0.0 collective-permute-start.1
  220.3 0.0 copy-start
  220.3 26.5 %adamw_1_0.1 = (bf16[2,768,2304]{2,1,0:T(8,128)(2,1)}, bf16[2,768,2304]{2,1,0:T(8,128)(2,1)}, bf16[2,2304,768]{2,1,0:T(8,128)(2,1)}, f32[2,768,2304]{2,1,0:T(8,1...) custom-call(s32[1]{0:T(128)} %constant.57.clone.1.rows_ref, ...), custom_call_target="tpu_custom_call" | custom-call | flops 33333334016 | bytes 78000000 | tf_op jit(solution)/shard_map/adamw_1_0/pallas_call | solution.py:569
  246.8 0.0 collective-permute-done.3.refs_5_
  246.8 0.0 copy-done
  246.8 1.0 collective-permute-start.7
  247.9 0.0 collective-permute-done.refs_2_
  247.9 0.0 collective-permute-done.2.refs_4_
  247.9 1.4 collective-permute-done.1.refs_3_
  249.2 1.1 collective-permute-start.9
  250.4 0.0 collective-permute-start.4
  250.4 2.7 collective-permute-start.5
  253.0 15.8 %adamw_1_2.1 = (bf16[2,768,2304]{2,1,0:T(8,128)(2,1)}, bf16[2,768,2304]{2,1,0:T(8,128)(2,1)}, bf16[2,2304,768]{2,1,0:T(8,128)(2,1)}, f32[2,768,2304]{2,1,0:T(8,1...) custom-call(s32[1]{0:T(128)} %constant.57.clone.1.rows_ref, ...), custom_call_target="tpu_custom_call", output_to_operand_aliasing={{0}: (12, {}), {1}: (13, {}), {2}: (14, {}), {3}: (15, {}),... | custom-call | flops 16666667008 | bytes 39000000 | tf_op jit(solution)/shard_map/adamw_1_2/pallas_call | solution.py:569
  268.8 0.0 collective-permute-done.4.refs_6_
  268.8 0.6 collective-permute-start.8
  269.4 0.0 collective-permute-done.5.refs_7_
  269.4 0.1 collective-permute-start.10
  269.6 0.0 collective-permute-done.6.refs_8_
  269.6 0.4 collective-permute-start.11
  270.0 0.0 collective-permute-done.7.refs_9_
  270.0 0.1 collective-permute-start.12
  270.1 0.0 collective-permute-done.9.refs_11_
  270.1 0.4 collective-permute-start.13
  270.5 0.7 stack.67.rows_ref
  271.1 1.9 collective-permute-done.11.refs_13_
  273.1 0.0 collective-permute-done.8.refs_10_
  273.1 0.0 collective-permute-done.10.refs_12_
  273.1 0.9 collective-permute-done.12.refs_14_
  274.0 0.0 copy-start.1
  274.0 0.9 collective-permute-done.13.refs_15_
  275.0 0.0 copy-done.1
  275.0 40.2 %adamw_0_0.1 = (bf16[2,768,2304]{2,1,0:T(8,128)(2,1)}, bf16[2,768,2304]{2,1,0:T(8,128)(2,1)}, bf16[2,2304,768]{2,1,0:T(8,128)(2,1)}, f32[2,768,2304]{2,1,0:T(8,1...) custom-call(s32[16]{0:T(128)} %stack.67.rows_ref, ...), custom_call_target="tpu_custom_call", output_to_operand_aliasing={{0}: (27, {}), {1}: (28, {}), {2}: (29, {}), {3}: (30, {}),... | custom-call | flops 49999998976 | bytes 117000000 | tf_op jit(solution)/shard_map/adamw_0_0/pallas_call | solution.py:569
Async XLA Ops:
  215.5 54.1 %collective-permute-start.6 = (bf16[9,48,768]{2,1,0:T(8,128)(2,1)}, bf16[9,48,768]{2,1,0:T(8,128)(2,1)}, u32[]{:S(2)}, u32[]{:S(2)}) collective-permute-start(bf16[9,48,768]{2,1,0:T(8,128)(2,1)} %get-tuple-element.69.refs_0_), channel_id=1, source_target_pairs={{0,1},{1,0},{2,3},{3,2},{4,5},{5,4},{6,7},{7,6},{8,9},{9,8},{10,11... | collective-permute-start | bytes 1990664 | tf_op jit(solution)/shard_map/ppermute | solution.py:597
  216.3 30.5 %collective-permute-start.3 = (bf16[9,48,768]{2,1,0:T(8,128)(2,1)}, bf16[9,48,768]{2,1,0:T(8,128)(2,1)}, u32[]{:S(2)}, u32[]{:S(2)}) collective-permute-start(bf16[9,48,768]{2,1,0:T(8,128)(2,1)} %get-tuple-element.69.refs_0_), channel_id=1, source_target_pairs={{0,6},{1,7},{2,0},{3,1},{4,2},{5,3},{6,4},{7,5},{8,14},{9,15},{10,... | collective-permute-start | bytes 1990664 | tf_op jit(solution)/shard_map/ppermute | solution.py:594
  217.6 30.3 %collective-permute-start = (bf16[9,48,768]{2,1,0:T(8,128)(2,1)}, bf16[9,48,768]{2,1,0:T(8,128)(2,1)}, u32[]{:S(2)}, u32[]{:S(2)}) collective-permute-start(bf16[9,48,768]{2,1,0:T(8,128)(2,1)} %get-tuple-element.69.refs_0_), channel_id=1, source_target_pairs={{0,2},{1,3},{2,4},{3,5},{4,6},{5,7},{6,0},{7,1},{8,10},{9,11},{10,... | collective-permute-start | bytes 1990664 | tf_op jit(solution)/shard_map/ppermute | solution.py:594
  217.8 30.1 %collective-permute-start.2 = (bf16[9,48,768]{2,1,0:T(8,128)(2,1)}, bf16[9,48,768]{2,1,0:T(8,128)(2,1)}, u32[]{:S(2)}, u32[]{:S(2)}) collective-permute-start(bf16[9,48,768]{2,1,0:T(8,128)(2,1)} %get-tuple-element.70.refs_1_), channel_id=1, source_target_pairs={{0,6},{1,7},{2,0},{3,1},{4,2},{5,3},{6,4},{7,5},{8,14},{9,15},{10,... | collective-permute-start | bytes 1990664 | tf_op jit(solution)/shard_map/ppermute | solution.py:594
  220.3 28.9 %collective-permute-start.1 = (bf16[9,48,768]{2,1,0:T(8,128)(2,1)}, bf16[9,48,768]{2,1,0:T(8,128)(2,1)}, u32[]{:S(2)}, u32[]{:S(2)}) collective-permute-start(bf16[9,48,768]{2,1,0:T(8,128)(2,1)} %get-tuple-element.70.refs_1_), channel_id=1, source_target_pairs={{0,2},{1,3},{2,4},{3,5},{4,6},{5,7},{6,0},{7,1},{8,10},{9,11},{10,... | collective-permute-start | bytes 1990664 | tf_op jit(solution)/shard_map/ppermute | solution.py:594
  220.3 26.5 %copy-start = (bf16[9,48,768]{2,1,0:T(8,128)(2,1)S(1)}, bf16[9,48,768]{2,1,0:T(8,128)(2,1)}, u32[]{:S(2)}) copy-start(bf16[9,48,768]{2,1,0:T(8,128)(2,1)} %get-tuple-element.70.refs_1_) | copy-start | bytes 1990660
  246.8 23.1 %collective-permute-start.7 = (bf16[9,48,768]{2,1,0:T(8,128)(2,1)S(1)}, bf16[9,48,768]{2,1,0:T(8,128)(2,1)}, u32[]{:S(2)}, u32[]{:S(2)}) collective-permute-start(bf16[9,48,768]{2,1,0:T(8,128)(2,1)S(1)} %copy-done), channel_id=1, source_target_pairs={{0,1},{1,0},{2,3},{3,2},{4,5},{5,4},{6,7},{7,6},{8,9},{9,8},{10,11... | collective-permute-start | bytes 1990664 | tf_op jit(solution)/shard_map/ppermute | solution.py:597
  249.2 20.9 %collective-permute-start.9 = (bf16[9,48,768]{2,1,0:T(8,128)(2,1)}, bf16[9,48,768]{2,1,0:T(8,128)(2,1)}, u32[]{:S(2)}, u32[]{:S(2)}) collective-permute-start(bf16[9,48,768]{2,1,0:T(8,128)(2,1)} %collective-permute-done.1.refs_3_), channel_id=1, source_target_pairs={{0,1},{1,0},{2,3},{3,2},{4,5},{5,4},{6,7},{7,6},{8,9},{9,8},{10,11... | collective-permute-start | bytes 1990664 | tf_op jit(solution)/shard_map/ppermute | solution.py:597
  250.4 18.5 %collective-permute-start.4 = (bf16[9,48,768]{2,1,0:T(8,128)(2,1)}, bf16[9,48,768]{2,1,0:T(8,128)(2,1)}, u32[]{:S(2)}, u32[]{:S(2)}) collective-permute-start(bf16[9,48,768]{2,1,0:T(8,128)(2,1)} %collective-permute-done.refs_2_), channel_id=1, source_target_pairs={{0,2},{1,3},{2,4},{3,5},{4,6},{5,7},{6,0},{7,1},{8,10},{9,11},{10,... | collective-permute-start | bytes 1990664 | tf_op jit(solution)/shard_map/ppermute | solution.py:594
  250.4 19.1 %collective-permute-start.5 = (bf16[9,48,768]{2,1,0:T(8,128)(2,1)}, bf16[9,48,768]{2,1,0:T(8,128)(2,1)}, u32[]{:S(2)}, u32[]{:S(2)}) collective-permute-start(bf16[9,48,768]{2,1,0:T(8,128)(2,1)} %collective-permute-done.2.refs_4_), channel_id=1, source_target_pairs={{0,6},{1,7},{2,0},{3,1},{4,2},{5,3},{6,4},{7,5},{8,14},{9,15},{10,... | collective-permute-start | bytes 1990664 | tf_op jit(solution)/shard_map/ppermute | solution.py:594
  268.8 4.3 %collective-permute-start.8 = (bf16[9,48,768]{2,1,0:T(8,128)(2,1)}, bf16[9,48,768]{2,1,0:T(8,128)(2,1)}, u32[]{:S(2)}, u32[]{:S(2)}) collective-permute-start(bf16[9,48,768]{2,1,0:T(8,128)(2,1)} %collective-permute-done.refs_2_), channel_id=1, source_target_pairs={{0,1},{1,0},{2,3},{3,2},{4,5},{5,4},{6,7},{7,6},{8,9},{9,8},{10,11... | collective-permute-start | bytes 1990664 | tf_op jit(solution)/shard_map/ppermute | solution.py:597
  269.4 3.6 %collective-permute-start.10 = (bf16[9,48,768]{2,1,0:T(8,128)(2,1)}, bf16[9,48,768]{2,1,0:T(8,128)(2,1)}, u32[]{:S(2)}, u32[]{:S(2)}) collective-permute-start(bf16[9,48,768]{2,1,0:T(8,128)(2,1)} %collective-permute-done.2.refs_4_), channel_id=1, source_target_pairs={{0,1},{1,0},{2,3},{3,2},{4,5},{5,4},{6,7},{7,6},{8,9},{9,8},{10,11... | collective-permute-start | bytes 1990664 | tf_op jit(solution)/shard_map/ppermute | solution.py:597
  269.6 3.5 %collective-permute-start.11 = (bf16[9,48,768]{2,1,0:T(8,128)(2,1)}, bf16[9,48,768]{2,1,0:T(8,128)(2,1)}, u32[]{:S(2)}, u32[]{:S(2)}) collective-permute-start(bf16[9,48,768]{2,1,0:T(8,128)(2,1)} %collective-permute-done.3.refs_5_), channel_id=1, source_target_pairs={{0,1},{1,0},{2,3},{3,2},{4,5},{5,4},{6,7},{7,6},{8,9},{9,8},{10,11... | collective-permute-start | bytes 1990664 | tf_op jit(solution)/shard_map/ppermute | solution.py:597
  270.0 4.1 %collective-permute-start.12 = (bf16[9,48,768]{2,1,0:T(8,128)(2,1)}, bf16[9,48,768]{2,1,0:T(8,128)(2,1)S(1)}, u32[]{:S(2)}, u32[]{:S(2)}) collective-permute-start(bf16[9,48,768]{2,1,0:T(8,128)(2,1)} %collective-permute-done.4.refs_6_), channel_id=1, source_target_pairs={{0,1},{1,0},{2,3},{3,2},{4,5},{5,4},{6,7},{7,6},{8,9},{9,8},{10,11... | collective-permute-start | bytes 1990664 | tf_op jit(solution)/shard_map/ppermute | solution.py:597
  270.1 4.9 %collective-permute-start.13 = (bf16[9,48,768]{2,1,0:T(8,128)(2,1)}, bf16[9,48,768]{2,1,0:T(8,128)(2,1)}, u32[]{:S(2)}, u32[]{:S(2)}) collective-permute-start(bf16[9,48,768]{2,1,0:T(8,128)(2,1)} %collective-permute-done.5.refs_7_), channel_id=1, source_target_pairs={{0,1},{1,0},{2,3},{3,2},{4,5},{5,4},{6,7},{7,6},{8,9},{9,8},{10,11... | collective-permute-start | bytes 1990664 | tf_op jit(solution)/shard_map/ppermute | solution.py:597
  274.0 1.0 copy-start.1

commit v5 on v4

--- a/solution.py
+++ b/solution.py
@@ -10,7 +10,7 @@
 F32, BF16 = jnp.float32, jnp.bfloat16
 MESH = pl.DeviceIdType.MESH
 WIDTH = 768
-STRIP = 256
+STRIP = 384
 CHUNK = 512
 SLOTS = 6
 VMEM_LIMIT = 63 * 1024 * 1024
@@ -144,6 +144,7 @@
         peers = [(self.chip, 1 - self.core), (self.right, self.core), (self.left, self.core)]
         if far:
             peers.append((self.far, self.core))
+            peers += [(chip, 1 - self.core) for chip in (self.right, self.left, self.far)]
         for peer in peers:
             pl.semaphore_signal(barrier, inc=1, device_id=self.to(*peer), device_id_type=MESH)
         pl.semaphore_wait(barrier, len(peers))
@@ -278,29 +279,28 @@
 
 
 def squares_over_group(ex, squares_ref, slots, sems):
-    def send(slot, which, chip, core):
+    me = ex.chip * 2 + ex.core
+    n = 2 * ex.chips
+
+    def send(i):
         return pltpu.make_async_remote_copy(
-            src_ref=slots.at[slot],
-            dst_ref=slots.at[5 if which == 0 else 1 + ex.chip],
-            send_sem=sems.at[0, which],
-            recv_sem=sems.at[1, which],
-            device_id=ex.to(chip, core),
+            src_ref=squares_ref,
+            dst_ref=slots.at[me],
+            send_sem=sems.at[0, i],
+            recv_sem=sems.at[1, i],
+            device_id={"dp": lax.rem(me + i, n)},
             device_id_type=MESH,
         )
 
-    slots[0] = squares_ref[...]
-    swap = send(0, 0, ex.chip, 1 - ex.core)
-    swap.start()
-    swap.wait()
-    slots[1 + ex.chip] = slots[0] + slots[5]
-    copies = [send(1 + ex.chip, 1 + i, chip, ex.core) for i, chip in enumerate((ex.right, ex.left, ex.far))]
+    copies = [send(i) for i in range(1, n)]
     for copy in copies:
         copy.start()
+    slots[me] = squares_ref[...]
     for copy in copies:
         copy.wait()
-    total = slots[1]
-    for chip in range(1, ex.chips):
-        total = total + slots[1 + chip]
+    total = slots[0]
+    for i in range(1, n):
+        total = total + slots[i]
     squares_ref[...] = total
 
 
@@ -454,10 +454,11 @@
                 dh_ref[0, rows, :] = dy_ref[0, rows, :] + through.astype(BF16)
                 return 0
 
-            lax.fori_loop(0, steps, by_h, 0)
-        if with_da:
+            lax.fori_loop(0, steps // 2, by_h, 0)
+            due(here, "s2t0")
+            lax.fori_loop(steps // 2, steps, by_h, 0)
             due(before, "404142")
-            due(here, "s2t0t1t2")
+            due(here, "t1t2")
         else:
             due(before, "t1")
             due(here, "s0f2")
@@ -504,12 +505,12 @@
             pltpu.VMEM((units, chips * share, WIDTH), BF16),
             pltpu.VMEM((units, 2, share // 2, WIDTH), BF16),
             pltpu.VMEM((units, 2, share, WIDTH), BF16),
-            pltpu.VMEM((chips + 2, 8, 128), F32),
+            pltpu.VMEM((n, 8, 128), F32),
             pltpu.SemaphoreType.DMA((2, units)),
             pltpu.SemaphoreType.DMA((2, units, 6)),
             pltpu.SemaphoreType.DMA((2, gathered, 9)),
             pltpu.SemaphoreType.DMA((gathered,)),
-            pltpu.SemaphoreType.DMA((2, 4)),
+            pltpu.SemaphoreType.DMA((2, n)),
         ],
         compiler_params=pltpu.CompilerParams(
             vmem_limit_bytes=VMEM_LIMIT, dimension_semantics=("arbitrary",), collective_id=1 + layer, has_side_effects=True

time: 316 us -> 313 us (level)
  transfers between devices with their start and end apart: 14 -> 14, of which waited for: 4 -> 5; matrix products, arithmetic and copies ran while one was open for 0% -> 0% of each run, Pallas kernels for 13% -> 13%
where the time goes in v5:
time: 313 us
  Pallas kernels  295 us (94%)
  starting transfers between devices  11.1 us (4%)
  waiting for transfers between devices  4.99 us (2%)
    pallas_call x2, Pallas kernels, backward(): pl.pallas_call(functools.partial(backward_kernel, n, with_da), grid=(ff /...  181 us
    pallas_call x3, Pallas kernels, adamw(): pl.pallas_call(kernel, grid=(parts * strips,), in_specs=[pl.BlockSpec(mem...  80.7 us
    pallas_call x1, Pallas kernels, forward(): pl.pallas_call(forward_kernel, grid=(ff // WIDTH,), in_specs=[once(h.shap...  33.3 us
    ppermute x6, starting transfers between devices, shift(): lax.ppermute(a, 'dp', [(c * 2 + k, (c + by) % chips * 2 + k) for c in ran...  6.71 us
  transfers between devices with their start and end apart: 14, of which 5 were waited for; matrix products, arithmetic and copies ran while one was open for 0% of the time, Pallas kernels for 13%

profile of v5, /device:TPU:113, one launch (start us, length us, event | category | flops | bytes accessed | tf_op | source)
XLA Modules:
  0.0 312.7 jit_solution(11906349176538566968)
XLA Ops:
  0.6 33.3 %forward.1 = (bf16[1,2048,768]{2,1,0:T(8,128)(2,1)}, f32[3,2048,768]{2,1,0:T(8,128)}, f32[3,2048,768]{2,1,0:T(8,128)}) custom-call(bf16[1,2048,768]{2,1,0:T(8,128)(2,1)} %h_ref.3, bf16[2,768,2304]{2,1,0:T(8,128)(2,1)} %refs_16_.1, bf16[2,768,2304]{2,1,0:T(8,128)(2,1)} %refs_17_.1, bf16[2,2304,768]{2,1,0:T(8,128)(2,1)} %refs_18_.1), custom_call_target="tpu_custom_call" | custom-call | tf_op jit(solution)/shard_map/forward/pallas_call | solution.py:108
  33.9 103.7 %backward_1.1 = (f32[8,128]{1,0:T(8,128)}, bf16[6,768,768]{2,1,0:T(8,128)(2,1)}, bf16[9,96,768]{2,1,0:T(8,128)(2,1)}, bf16[1,2048,768]{2,1,0:T(8,128)(2,1)}) custom-call(bf16[1,2048,768]{2,1,0:T(8,128)(2,1)} %get-tuple-element.62.h_ref, bf16[1,2048,768]{2,1,0:T(8,128)(2,1)} %dy_ref.1, bf16[2,768,2304]{2,1,0:T(8,128)(2,1)} %refs_16_.1, ...), custom_call_target="tpu_custom_call" | custom-call | tf_op jit(solution)/shard_map/backward_1/pallas_call | solution.py:494
  137.6 77.4 %backward_0.1 = (f32[8,128]{1,0:T(8,128)}, bf16[3,768,768]{2,1,0:T(8,128)(2,1)}, bf16[9,48,768]{2,1,0:T(8,128)(2,1)}, bf16[9,48,768]{2,1,0:T(8,128)(2,1)}) custom-call(bf16[1,2048,768]{2,1,0:T(8,128)(2,1)} %h_ref.3, bf16[1,2048,768]{2,1,0:T(8,128)(2,1)} %get-tuple-element.63.dy_ref, bf16[2,2304,768]{2,1,0:T(8,128)(2,1)} %refs_18_.1, ...), custom_call_target="tpu_custom_call" | custom-call | tf_op jit(solution)/shard_map/backward_0/pallas_call | solution.py:494
  215.0 0.5 collective-permute-start.6
  215.5 1.4 collective-permute-start.3
  216.8 0.1 collective-permute-start
  216.9 2.6 collective-permute-start.2
  219.5 0.0 collective-permute-start.1
  219.5 0.0 copy-start
  219.5 27.2 %adamw_1_0.1 = (bf16[2,768,2304]{2,1,0:T(8,128)(2,1)}, bf16[2,768,2304]{2,1,0:T(8,128)(2,1)}, bf16[2,2304,768]{2,1,0:T(8,128)(2,1)}, f32[2,768,2304]{2,1,0:T(8,1...) custom-call(s32[1]{0:T(128)} %constant.57.clone.1.rows_ref, ...), custom_call_target="tpu_custom_call" | custom-call | flops 33333334016 | bytes 78000000 | tf_op jit(solution)/shard_map/adamw_1_0/pallas_call | solution.py:570
  246.8 0.0 collective-permute-done.3.refs_5_
  246.8 0.0 copy-done
  246.8 1.0 collective-permute-start.7
  247.8 0.0 collective-permute-done.refs_2_
  247.8 0.0 collective-permute-done.2.refs_4_
  247.8 0.6 collective-permute-done.1.refs_3_
  248.4 1.1 collective-permute-start.9
  249.6 0.0 collective-permute-start.4
  249.6 2.7 collective-permute-start.5
  252.3 14.6 %adamw_1_2.1 = (bf16[2,768,2304]{2,1,0:T(8,128)(2,1)}, bf16[2,768,2304]{2,1,0:T(8,128)(2,1)}, bf16[2,2304,768]{2,1,0:T(8,128)(2,1)}, f32[2,768,2304]{2,1,0:T(8,1...) custom-call(s32[1]{0:T(128)} %constant.57.clone.1.rows_ref, ...), custom_call_target="tpu_custom_call", output_to_operand_aliasing={{0}: (12, {}), {1}: (13, {}), {2}: (14, {}), {3}: (15, {}),... | custom-call | flops 16666667008 | bytes 39000000 | tf_op jit(solution)/shard_map/adamw_1_2/pallas_call | solution.py:570
  266.9 0.5 collective-permute-done.4.refs_6_
  267.4 0.8 collective-permute-start.8
  268.1 0.0 collective-permute-done.5.refs_7_
  268.1 0.0 collective-permute-start.10
  268.1 0.0 collective-permute-done.6.refs_8_
  268.1 0.5 collective-permute-start.11
  268.6 0.0 collective-permute-done.7.refs_9_
  268.6 0.1 collective-permute-start.12
  268.7 0.0 collective-permute-done.9.refs_11_
  268.7 0.4 collective-permute-start.13
  269.2 0.7 stack.67.rows_ref
  269.8 1.9 collective-permute-done.11.refs_13_
  271.8 0.0 collective-permute-done.8.refs_10_
  271.8 0.0 collective-permute-done.10.refs_12_
  271.8 0.9 collective-permute-done.12.refs_14_
  272.7 0.0 copy-start.1
  272.7 0.9 collective-permute-done.13.refs_15_
  273.7 0.0 copy-done.1
  273.7 38.8 %adamw_0_0.1 = (bf16[2,768,2304]{2,1,0:T(8,128)(2,1)}, bf16[2,768,2304]{2,1,0:T(8,128)(2,1)}, bf16[2,2304,768]{2,1,0:T(8,128)(2,1)}, f32[2,768,2304]{2,1,0:T(8,1...) custom-call(s32[16]{0:T(128)} %stack.67.rows_ref, ...), custom_call_target="tpu_custom_call", output_to_operand_aliasing={{0}: (27, {}), {1}: (28, {}), {2}: (29, {}), {3}: (30, {}),... | custom-call | flops 49999998976 | bytes 117000000 | tf_op jit(solution)/shard_map/adamw_0_0/pallas_call | solution.py:570
Async XLA Ops:
  215.0 53.1 %collective-permute-start.6 = (bf16[9,48,768]{2,1,0:T(8,128)(2,1)}, bf16[9,48,768]{2,1,0:T(8,128)(2,1)}, u32[]{:S(2)}, u32[]{:S(2)}) collective-permute-start(bf16[9,48,768]{2,1,0:T(8,128)(2,1)} %get-tuple-element.69.refs_0_), channel_id=1, source_target_pairs={{0,1},{1,0},{2,3},{3,2},{4,5},{5,4},{6,7},{7,6},{8,9},{9,8},{10,11... | collective-permute-start | bytes 1990664 | tf_op jit(solution)/shard_map/ppermute | solution.py:598
  215.5 31.3 %collective-permute-start.3 = (bf16[9,48,768]{2,1,0:T(8,128)(2,1)}, bf16[9,48,768]{2,1,0:T(8,128)(2,1)}, u32[]{:S(2)}, u32[]{:S(2)}) collective-permute-start(bf16[9,48,768]{2,1,0:T(8,128)(2,1)} %get-tuple-element.69.refs_0_), channel_id=1, source_target_pairs={{0,6},{1,7},{2,0},{3,1},{4,2},{5,3},{6,4},{7,5},{8,14},{9,15},{10,... | collective-permute-start | bytes 1990664 | tf_op jit(solution)/shard_map/ppermute | solution.py:595
  216.8 31.0 %collective-permute-start = (bf16[9,48,768]{2,1,0:T(8,128)(2,1)}, bf16[9,48,768]{2,1,0:T(8,128)(2,1)}, u32[]{:S(2)}, u32[]{:S(2)}) collective-permute-start(bf16[9,48,768]{2,1,0:T(8,128)(2,1)} %get-tuple-element.69.refs_0_), channel_id=1, source_target_pairs={{0,2},{1,3},{2,4},{3,5},{4,6},{5,7},{6,0},{7,1},{8,10},{9,11},{10,... | collective-permute-start | bytes 1990664 | tf_op jit(solution)/shard_map/ppermute | solution.py:595
  216.9 30.9 %collective-permute-start.2 = (bf16[9,48,768]{2,1,0:T(8,128)(2,1)}, bf16[9,48,768]{2,1,0:T(8,128)(2,1)}, u32[]{:S(2)}, u32[]{:S(2)}) collective-permute-start(bf16[9,48,768]{2,1,0:T(8,128)(2,1)} %get-tuple-element.70.refs_1_), channel_id=1, source_target_pairs={{0,6},{1,7},{2,0},{3,1},{4,2},{5,3},{6,4},{7,5},{8,14},{9,15},{10,... | collective-permute-start | bytes 1990664 | tf_op jit(solution)/shard_map/ppermute | solution.py:595
  219.5 28.9 %collective-permute-start.1 = (bf16[9,48,768]{2,1,0:T(8,128)(2,1)}, bf16[9,48,768]{2,1,0:T(8,128)(2,1)}, u32[]{:S(2)}, u32[]{:S(2)}) collective-permute-start(bf16[9,48,768]{2,1,0:T(8,128)(2,1)} %get-tuple-element.70.refs_1_), channel_id=1, source_target_pairs={{0,2},{1,3},{2,4},{3,5},{4,6},{5,7},{6,0},{7,1},{8,10},{9,11},{10,... | collective-permute-start | bytes 1990664 | tf_op jit(solution)/shard_map/ppermute | solution.py:595
  219.5 27.3 %copy-start = (bf16[9,48,768]{2,1,0:T(8,128)(2,1)S(1)}, bf16[9,48,768]{2,1,0:T(8,128)(2,1)}, u32[]{:S(2)}) copy-start(bf16[9,48,768]{2,1,0:T(8,128)(2,1)} %get-tuple-element.70.refs_1_) | copy-start | bytes 1990660
  246.8 21.9 %collective-permute-start.7 = (bf16[9,48,768]{2,1,0:T(8,128)(2,1)S(1)}, bf16[9,48,768]{2,1,0:T(8,128)(2,1)}, u32[]{:S(2)}, u32[]{:S(2)}) collective-permute-start(bf16[9,48,768]{2,1,0:T(8,128)(2,1)S(1)} %copy-done), channel_id=1, source_target_pairs={{0,1},{1,0},{2,3},{3,2},{4,5},{5,4},{6,7},{7,6},{8,9},{9,8},{10,11... | collective-permute-start | bytes 1990664 | tf_op jit(solution)/shard_map/ppermute | solution.py:598
  248.4 20.3 %collective-permute-start.9 = (bf16[9,48,768]{2,1,0:T(8,128)(2,1)}, bf16[9,48,768]{2,1,0:T(8,128)(2,1)}, u32[]{:S(2)}, u32[]{:S(2)}) collective-permute-start(bf16[9,48,768]{2,1,0:T(8,128)(2,1)} %collective-permute-done.1.refs_3_), channel_id=1, source_target_pairs={{0,1},{1,0},{2,3},{3,2},{4,5},{5,4},{6,7},{7,6},{8,9},{9,8},{10,11... | collective-permute-start | bytes 1990664 | tf_op jit(solution)/shard_map/ppermute | solution.py:598
  249.6 17.8 %collective-permute-start.4 = (bf16[9,48,768]{2,1,0:T(8,128)(2,1)}, bf16[9,48,768]{2,1,0:T(8,128)(2,1)}, u32[]{:S(2)}, u32[]{:S(2)}) collective-permute-start(bf16[9,48,768]{2,1,0:T(8,128)(2,1)} %collective-permute-done.refs_2_), channel_id=1, source_target_pairs={{0,2},{1,3},{2,4},{3,5},{4,6},{5,7},{6,0},{7,1},{8,10},{9,11},{10,... | collective-permute-start | bytes 1990664 | tf_op jit(solution)/shard_map/ppermute | solution.py:595
  249.6 18.5 %collective-permute-start.5 = (bf16[9,48,768]{2,1,0:T(8,128)(2,1)}, bf16[9,48,768]{2,1,0:T(8,128)(2,1)}, u32[]{:S(2)}, u32[]{:S(2)}) collective-permute-start(bf16[9,48,768]{2,1,0:T(8,128)(2,1)} %collective-permute-done.2.refs_4_), channel_id=1, source_target_pairs={{0,6},{1,7},{2,0},{3,1},{4,2},{5,3},{6,4},{7,5},{8,14},{9,15},{10,... | collective-permute-start | bytes 1990664 | tf_op jit(solution)/shard_map/ppermute | solution.py:595
  267.4 4.4 %collective-permute-start.8 = (bf16[9,48,768]{2,1,0:T(8,128)(2,1)}, bf16[9,48,768]{2,1,0:T(8,128)(2,1)}, u32[]{:S(2)}, u32[]{:S(2)}) collective-permute-start(bf16[9,48,768]{2,1,0:T(8,128)(2,1)} %collective-permute-done.refs_2_), channel_id=1, source_target_pairs={{0,1},{1,0},{2,3},{3,2},{4,5},{5,4},{6,7},{7,6},{8,9},{9,8},{10,11... | collective-permute-start | bytes 1990664 | tf_op jit(solution)/shard_map/ppermute | solution.py:598
  268.1 3.6 %collective-permute-start.10 = (bf16[9,48,768]{2,1,0:T(8,128)(2,1)}, bf16[9,48,768]{2,1,0:T(8,128)(2,1)}, u32[]{:S(2)}, u32[]{:S(2)}) collective-permute-start(bf16[9,48,768]{2,1,0:T(8,128)(2,1)} %collective-permute-done.2.refs_4_), channel_id=1, source_target_pairs={{0,1},{1,0},{2,3},{3,2},{4,5},{5,4},{6,7},{7,6},{8,9},{9,8},{10,11... | collective-permute-start | bytes 1990664 | tf_op jit(solution)/shard_map/ppermute | solution.py:598
  268.1 3.6 %collective-permute-start.11 = (bf16[9,48,768]{2,1,0:T(8,128)(2,1)}, bf16[9,48,768]{2,1,0:T(8,128)(2,1)}, u32[]{:S(2)}, u32[]{:S(2)}) collective-permute-start(bf16[9,48,768]{2,1,0:T(8,128)(2,1)} %collective-permute-done.3.refs_5_), channel_id=1, source_target_pairs={{0,1},{1,0},{2,3},{3,2},{4,5},{5,4},{6,7},{7,6},{8,9},{9,8},{10,11... | collective-permute-start | bytes 1990664 | tf_op jit(solution)/shard_map/ppermute | solution.py:598
  268.6 4.1 %collective-permute-start.12 = (bf16[9,48,768]{2,1,0:T(8,128)(2,1)}, bf16[9,48,768]{2,1,0:T(8,128)(2,1)S(1)}, u32[]{:S(2)}, u32[]{:S(2)}) collective-permute-start(bf16[9,48,768]{2,1,0:T(8,128)(2,1)} %collective-permute-done.4.refs_6_), channel_id=1, source_target_pairs={{0,1},{1,0},{2,3},{3,2},{4,5},{5,4},{6,7},{7,6},{8,9},{9,8},{10,11... | collective-permute-start | bytes 1990664 | tf_op jit(solution)/shard_map/ppermute | solution.py:598
  268.7 4.9 %collective-permute-start.13 = (bf16[9,48,768]{2,1,0:T(8,128)(2,1)}, bf16[9,48,768]{2,1,0:T(8,128)(2,1)}, u32[]{:S(2)}, u32[]{:S(2)}) collective-permute-start(bf16[9,48,768]{2,1,0:T(8,128)(2,1)} %collective-permute-done.5.refs_7_), channel_id=1, source_target_pairs={{0,1},{1,0},{2,3},{3,2},{4,5},{5,4},{6,7},{7,6},{8,9},{9,8},{10,11... | collective-permute-start | bytes 1990664 | tf_op jit(solution)/shard_map/ppermute | solution.py:598
  272.7 1.0 copy-start.1

commit v6 on v5

--- a/solution.py
+++ b/solution.py
@@ -460,9 +460,8 @@
             due(before, "404142")
             due(here, "t1t2")
         else:
-            due(before, "t1")
             due(here, "s0f2")
-            due(before, "t2")
+            due(before, "t1t2")
             due(here, "s1t0s2t1t2")
             squares_over_group(ex, squares_ref, slots, slot_sems)
 

time: 313 us -> 313 us (level)
  no operation moved by 1% of the time
where the time goes in v6:
time: 313 us
  Pallas kernels  295 us (94%)
  starting transfers between devices  11.1 us (4%)
  waiting for transfers between devices  4.99 us (2%)
    pallas_call x2, Pallas kernels, backward(): pl.pallas_call(functools.partial(backward_kernel, n, with_da), grid=(ff /...  181 us
    pallas_call x3, Pallas kernels, adamw(): pl.pallas_call(kernel, grid=(parts * strips,), in_specs=[pl.BlockSpec(mem...  80.7 us
    pallas_call x1, Pallas kernels, forward(): pl.pallas_call(forward_kernel, grid=(ff // WIDTH,), in_specs=[once(h.shap...  33.3 us
    ppermute x6, starting transfers between devices, shift(): lax.ppermute(a, 'dp', [(c * 2 + k, (c + by) % chips * 2 + k) for c in ran...  6.71 us
  transfers between devices with their start and end apart: 14, of which 5 were waited for; matrix products, arithmetic and copies ran while one was open for 0% of the time, Pallas kernels for 13%

profile of v6, /device:TPU:113, one launch (start us, length us, event | category | flops | bytes accessed | tf_op | source)
XLA Modules:
  0.0 312.7 jit_solution(15731904288939311865)
XLA Ops:
  0.6 33.3 %forward.1 = (bf16[1,2048,768]{2,1,0:T(8,128)(2,1)}, f32[3,2048,768]{2,1,0:T(8,128)}, f32[3,2048,768]{2,1,0:T(8,128)}) custom-call(bf16[1,2048,768]{2,1,0:T(8,128)(2,1)} %h_ref.3, bf16[2,768,2304]{2,1,0:T(8,128)(2,1)} %refs_16_.1, bf16[2,768,2304]{2,1,0:T(8,128)(2,1)} %refs_17_.1, bf16[2,2304,768]{2,1,0:T(8,128)(2,1)} %refs_18_.1), custom_call_target="tpu_custom_call" | custom-call | tf_op jit(solution)/shard_map/forward/pallas_call | solution.py:108
  33.9 103.7 %backward_1.1 = (f32[8,128]{1,0:T(8,128)}, bf16[6,768,768]{2,1,0:T(8,128)(2,1)}, bf16[9,96,768]{2,1,0:T(8,128)(2,1)}, bf16[1,2048,768]{2,1,0:T(8,128)(2,1)}) custom-call(bf16[1,2048,768]{2,1,0:T(8,128)(2,1)} %get-tuple-element.62.h_ref, bf16[1,2048,768]{2,1,0:T(8,128)(2,1)} %dy_ref.1, bf16[2,768,2304]{2,1,0:T(8,128)(2,1)} %refs_16_.1, ...), custom_call_target="tpu_custom_call" | custom-call | tf_op jit(solution)/shard_map/backward_1/pallas_call | solution.py:493
  137.6 77.4 %backward_0.1 = (f32[8,128]{1,0:T(8,128)}, bf16[3,768,768]{2,1,0:T(8,128)(2,1)}, bf16[9,48,768]{2,1,0:T(8,128)(2,1)}, bf16[9,48,768]{2,1,0:T(8,128)(2,1)}) custom-call(bf16[1,2048,768]{2,1,0:T(8,128)(2,1)} %h_ref.3, bf16[1,2048,768]{2,1,0:T(8,128)(2,1)} %get-tuple-element.63.dy_ref, bf16[2,2304,768]{2,1,0:T(8,128)(2,1)} %refs_18_.1, ...), custom_call_target="tpu_custom_call" | custom-call | tf_op jit(solution)/shard_map/backward_0/pallas_call | solution.py:493
  215.0 0.5 collective-permute-start.6
  215.5 1.4 collective-permute-start.3
  216.8 0.1 collective-permute-start
  216.9 2.6 collective-permute-start.2
  219.5 0.0 collective-permute-start.1
  219.5 0.0 copy-start
  219.5 27.2 %adamw_1_0.1 = (bf16[2,768,2304]{2,1,0:T(8,128)(2,1)}, bf16[2,768,2304]{2,1,0:T(8,128)(2,1)}, bf16[2,2304,768]{2,1,0:T(8,128)(2,1)}, f32[2,768,2304]{2,1,0:T(8,1...) custom-call(s32[1]{0:T(128)} %constant.57.clone.1.rows_ref, ...), custom_call_target="tpu_custom_call" | custom-call | flops 33333334016 | bytes 78000000 | tf_op jit(solution)/shard_map/adamw_1_0/pallas_call | solution.py:569
  246.8 0.0 collective-permute-done.3.refs_5_
  246.8 0.0 copy-done
  246.8 1.0 collective-permute-start.7
  247.8 0.0 collective-permute-done.refs_2_
  247.8 0.0 collective-permute-done.2.refs_4_
  247.8 0.6 collective-permute-done.1.refs_3_
  248.4 1.1 collective-permute-start.9
  249.6 0.0 collective-permute-start.4
  249.6 2.7 collective-permute-start.5
  252.3 14.6 %adamw_1_2.1 = (bf16[2,768,2304]{2,1,0:T(8,128)(2,1)}, bf16[2,768,2304]{2,1,0:T(8,128)(2,1)}, bf16[2,2304,768]{2,1,0:T(8,128)(2,1)}, f32[2,768,2304]{2,1,0:T(8,1...) custom-call(s32[1]{0:T(128)} %constant.57.clone.1.rows_ref, ...), custom_call_target="tpu_custom_call", output_to_operand_aliasing={{0}: (12, {}), {1}: (13, {}), {2}: (14, {}), {3}: (15, {}),... | custom-call | flops 16666667008 | bytes 39000000 | tf_op jit(solution)/shard_map/adamw_1_2/pallas_call | solution.py:569
  266.9 0.5 collective-permute-done.4.refs_6_
  267.4 0.8 collective-permute-start.8
  268.1 0.0 collective-permute-done.5.refs_7_
  268.1 0.0 collective-permute-start.10
  268.1 0.0 collective-permute-done.6.refs_8_
  268.1 0.5 collective-permute-start.11
  268.6 0.0 collective-permute-done.7.refs_9_
  268.6 0.1 collective-permute-start.12
  268.7 0.0 collective-permute-done.9.refs_11_
  268.7 0.4 collective-permute-start.13
  269.2 0.7 stack.67.rows_ref
  269.8 1.9 collective-permute-done.11.refs_13_
  271.8 0.0 collective-permute-done.8.refs_10_
  271.8 0.0 collective-permute-done.10.refs_12_
  271.8 0.9 collective-permute-done.12.refs_14_
  272.7 0.0 copy-start.1
  272.7 0.9 collective-permute-done.13.refs_15_
  273.7 0.0 copy-done.1
  273.7 38.8 %adamw_0_0.1 = (bf16[2,768,2304]{2,1,0:T(8,128)(2,1)}, bf16[2,768,2304]{2,1,0:T(8,128)(2,1)}, bf16[2,2304,768]{2,1,0:T(8,128)(2,1)}, f32[2,768,2304]{2,1,0:T(8,1...) custom-call(s32[16]{0:T(128)} %stack.67.rows_ref, ...), custom_call_target="tpu_custom_call", output_to_operand_aliasing={{0}: (27, {}), {1}: (28, {}), {2}: (29, {}), {3}: (30, {}),... | custom-call | flops 49999998976 | bytes 117000000 | tf_op jit(solution)/shard_map/adamw_0_0/pallas_call | solution.py:569
Async XLA Ops:
  215.0 53.1 %collective-permute-start.6 = (bf16[9,48,768]{2,1,0:T(8,128)(2,1)}, bf16[9,48,768]{2,1,0:T(8,128)(2,1)}, u32[]{:S(2)}, u32[]{:S(2)}) collective-permute-start(bf16[9,48,768]{2,1,0:T(8,128)(2,1)} %get-tuple-element.69.refs_0_), channel_id=1, source_target_pairs={{0,1},{1,0},{2,3},{3,2},{4,5},{5,4},{6,7},{7,6},{8,9},{9,8},{10,11... | collective-permute-start | bytes 1990664 | tf_op jit(solution)/shard_map/ppermute | solution.py:597
  215.5 31.3 %collective-permute-start.3 = (bf16[9,48,768]{2,1,0:T(8,128)(2,1)}, bf16[9,48,768]{2,1,0:T(8,128)(2,1)}, u32[]{:S(2)}, u32[]{:S(2)}) collective-permute-start(bf16[9,48,768]{2,1,0:T(8,128)(2,1)} %get-tuple-element.69.refs_0_), channel_id=1, source_target_pairs={{0,6},{1,7},{2,0},{3,1},{4,2},{5,3},{6,4},{7,5},{8,14},{9,15},{10,... | collective-permute-start | bytes 1990664 | tf_op jit(solution)/shard_map/ppermute | solution.py:594
  216.8 31.0 %collective-permute-start = (bf16[9,48,768]{2,1,0:T(8,128)(2,1)}, bf16[9,48,768]{2,1,0:T(8,128)(2,1)}, u32[]{:S(2)}, u32[]{:S(2)}) collective-permute-start(bf16[9,48,768]{2,1,0:T(8,128)(2,1)} %get-tuple-element.69.refs_0_), channel_id=1, source_target_pairs={{0,2},{1,3},{2,4},{3,5},{4,6},{5,7},{6,0},{7,1},{8,10},{9,11},{10,... | collective-permute-start | bytes 1990664 | tf_op jit(solution)/shard_map/ppermute | solution.py:594
  216.9 30.9 %collective-permute-start.2 = (bf16[9,48,768]{2,1,0:T(8,128)(2,1)}, bf16[9,48,768]{2,1,0:T(8,128)(2,1)}, u32[]{:S(2)}, u32[]{:S(2)}) collective-permute-start(bf16[9,48,768]{2,1,0:T(8,128)(2,1)} %get-tuple-element.70.refs_1_), channel_id=1, source_target_pairs={{0,6},{1,7},{2,0},{3,1},{4,2},{5,3},{6,4},{7,5},{8,14},{9,15},{10,... | collective-permute-start | bytes 1990664 | tf_op jit(solution)/shard_map/ppermute | solution.py:594
  219.5 28.9 %collective-permute-start.1 = (bf16[9,48,768]{2,1,0:T(8,128)(2,1)}, bf16[9,48,768]{2,1,0:T(8,128)(2,1)}, u32[]{:S(2)}, u32[]{:S(2)}) collective-permute-start(bf16[9,48,768]{2,1,0:T(8,128)(2,1)} %get-tuple-element.70.refs_1_), channel_id=1, source_target_pairs={{0,2},{1,3},{2,4},{3,5},{4,6},{5,7},{6,0},{7,1},{8,10},{9,11},{10,... | collective-permute-start | bytes 1990664 | tf_op jit(solution)/shard_map/ppermute | solution.py:594
  219.5 27.3 %copy-start = (bf16[9,48,768]{2,1,0:T(8,128)(2,1)S(1)}, bf16[9,48,768]{2,1,0:T(8,128)(2,1)}, u32[]{:S(2)}) copy-start(bf16[9,48,768]{2,1,0:T(8,128)(2,1)} %get-tuple-element.70.refs_1_) | copy-start | bytes 1990660
  246.8 21.9 %collective-permute-start.7 = (bf16[9,48,768]{2,1,0:T(8,128)(2,1)S(1)}, bf16[9,48,768]{2,1,0:T(8,128)(2,1)}, u32[]{:S(2)}, u32[]{:S(2)}) collective-permute-start(bf16[9,48,768]{2,1,0:T(8,128)(2,1)S(1)} %copy-done), channel_id=1, source_target_pairs={{0,1},{1,0},{2,3},{3,2},{4,5},{5,4},{6,7},{7,6},{8,9},{9,8},{10,11... | collective-permute-start | bytes 1990664 | tf_op jit(solution)/shard_map/ppermute | solution.py:597
  248.4 20.3 %collective-permute-start.9 = (bf16[9,48,768]{2,1,0:T(8,128)(2,1)}, bf16[9,48,768]{2,1,0:T(8,128)(2,1)}, u32[]{:S(2)}, u32[]{:S(2)}) collective-permute-start(bf16[9,48,768]{2,1,0:T(8,128)(2,1)} %collective-permute-done.1.refs_3_), channel_id=1, source_target_pairs={{0,1},{1,0},{2,3},{3,2},{4,5},{5,4},{6,7},{7,6},{8,9},{9,8},{10,11... | collective-permute-start | bytes 1990664 | tf_op jit(solution)/shard_map/ppermute | solution.py:597
  249.6 17.8 %collective-permute-start.4 = (bf16[9,48,768]{2,1,0:T(8,128)(2,1)}, bf16[9,48,768]{2,1,0:T(8,128)(2,1)}, u32[]{:S(2)}, u32[]{:S(2)}) collective-permute-start(bf16[9,48,768]{2,1,0:T(8,128)(2,1)} %collective-permute-done.refs_2_), channel_id=1, source_target_pairs={{0,2},{1,3},{2,4},{3,5},{4,6},{5,7},{6,0},{7,1},{8,10},{9,11},{10,... | collective-permute-start | bytes 1990664 | tf_op jit(solution)/shard_map/ppermute | solution.py:594
  249.6 18.5 %collective-permute-start.5 = (bf16[9,48,768]{2,1,0:T(8,128)(2,1)}, bf16[9,48,768]{2,1,0:T(8,128)(2,1)}, u32[]{:S(2)}, u32[]{:S(2)}) collective-permute-start(bf16[9,48,768]{2,1,0:T(8,128)(2,1)} %collective-permute-done.2.refs_4_), channel_id=1, source_target_pairs={{0,6},{1,7},{2,0},{3,1},{4,2},{5,3},{6,4},{7,5},{8,14},{9,15},{10,... | collective-permute-start | bytes 1990664 | tf_op jit(solution)/shard_map/ppermute | solution.py:594
  267.4 4.4 %collective-permute-start.8 = (bf16[9,48,768]{2,1,0:T(8,128)(2,1)}, bf16[9,48,768]{2,1,0:T(8,128)(2,1)}, u32[]{:S(2)}, u32[]{:S(2)}) collective-permute-start(bf16[9,48,768]{2,1,0:T(8,128)(2,1)} %collective-permute-done.refs_2_), channel_id=1, source_target_pairs={{0,1},{1,0},{2,3},{3,2},{4,5},{5,4},{6,7},{7,6},{8,9},{9,8},{10,11... | collective-permute-start | bytes 1990664 | tf_op jit(solution)/shard_map/ppermute | solution.py:597
  268.1 3.6 %collective-permute-start.10 = (bf16[9,48,768]{2,1,0:T(8,128)(2,1)}, bf16[9,48,768]{2,1,0:T(8,128)(2,1)}, u32[]{:S(2)}, u32[]{:S(2)}) collective-permute-start(bf16[9,48,768]{2,1,0:T(8,128)(2,1)} %collective-permute-done.2.refs_4_), channel_id=1, source_target_pairs={{0,1},{1,0},{2,3},{3,2},{4,5},{5,4},{6,7},{7,6},{8,9},{9,8},{10,11... | collective-permute-start | bytes 1990664 | tf_op jit(solution)/shard_map/ppermute | solution.py:597
  268.1 3.6 %collective-permute-start.11 = (bf16[9,48,768]{2,1,0:T(8,128)(2,1)}, bf16[9,48,768]{2,1,0:T(8,128)(2,1)}, u32[]{:S(2)}, u32[]{:S(2)}) collective-permute-start(bf16[9,48,768]{2,1,0:T(8,128)(2,1)} %collective-permute-done.3.refs_5_), channel_id=1, source_target_pairs={{0,1},{1,0},{2,3},{3,2},{4,5},{5,4},{6,7},{7,6},{8,9},{9,8},{10,11... | collective-permute-start | bytes 1990664 | tf_op jit(solution)/shard_map/ppermute | solution.py:597
  268.6 4.1 %collective-permute-start.12 = (bf16[9,48,768]{2,1,0:T(8,128)(2,1)}, bf16[9,48,768]{2,1,0:T(8,128)(2,1)S(1)}, u32[]{:S(2)}, u32[]{:S(2)}) collective-permute-start(bf16[9,48,768]{2,1,0:T(8,128)(2,1)} %collective-permute-done.4.refs_6_), channel_id=1, source_target_pairs={{0,1},{1,0},{2,3},{3,2},{4,5},{5,4},{6,7},{7,6},{8,9},{9,8},{10,11... | collective-permute-start | bytes 1990664 | tf_op jit(solution)/shard_map/ppermute | solution.py:597
  268.7 4.9 %collective-permute-start.13 = (bf16[9,48,768]{2,1,0:T(8,128)(2,1)}, bf16[9,48,768]{2,1,0:T(8,128)(2,1)}, u32[]{:S(2)}, u32[]{:S(2)}) collective-permute-start(bf16[9,48,768]{2,1,0:T(8,128)(2,1)} %collective-permute-done.5.refs_7_), channel_id=1, source_target_pairs={{0,1},{1,0},{2,3},{3,2},{4,5},{5,4},{6,7},{7,6},{8,9},{9,8},{10,11... | collective-permute-start | bytes 1990664 | tf_op jit(solution)/shard_map/ppermute | solution.py:597
  272.7 1.0 copy-start.1
